TPU v7x, 16 devices: a whole 2x2x2 slice. The times are simulated.
16 devices in a mesh: tp: 2 (over z), dp: 8 (over y, x, core).
Axes of the slice: x: 2, y: 2, z: 2, core: 2. Of those that a mesh axis runs over, the one named last changes fastest.
Arguments:
- x_in: bfloat16 [2, 128, 4096], P(None, ('dp', 'tp'))
- w_gate: bfloat16 [4096, 11008], P('dp', 'tp')
- w_up: bfloat16 [4096, 11008], P('dp', 'tp')
- w_down: bfloat16 [11008, 4096], P('tp', 'dp')
- grad_y: bfloat16 [2, 128, 4096], P(None, ('dp', 'tp'))
Outputs:
- output 1: bfloat16 [2, 128, 4096], P(None, ('dp', 'tp'))
- output 2: bfloat16 [2, 128, 4096], P(None, ('dp', 'tp'))
- output 3: float32 [4096, 11008], P('dp', 'tp')
- output 4: float32 [4096, 11008], P('dp', 'tp')
- output 5: float32 [11008, 4096], P('tp', 'dp')
All inputs are finite; a program needn't handle non-finite values.
Results may differ from a plain program's by a relative error of at most 0.001.
Values are sent between devices in bfloat16 or wider.
A program may use at most 1 GiB of HBM per device.

v0:
```python
import jax
import jax.numpy as jnp
from jax import lax
from jax.sharding import PartitionSpec as P


def gate_grads(grad_h, gate_pre, up_pre, sig_gate, act_gate):
    grad_gate = grad_h * up_pre * sig_gate * (1.0 + gate_pre * (1.0 - sig_gate))
    grad_up = grad_h * act_gate
    return grad_gate.astype(jnp.bfloat16), grad_up.astype(jnp.bfloat16)


def solution(mesh):
    data_size = mesh.shape["dp"]
    model_size = mesh.shape["tp"]
    row_spec = P(None, ("dp", "tp"), None)
    in_specs = (row_spec, P("dp", "tp"), P("dp", "tp"), P("tp", "dp"), row_spec)
    out_specs = (row_spec, row_spec, P("dp", "tp"), P("dp", "tp"), P("tp", "dp"))

    def token_columns(rows_loc):
        spread = lax.all_to_all(rows_loc, "dp", split_axis=1, concat_axis=0, tiled=True)
        gathered = lax.all_gather(spread, "tp", axis=0)
        return gathered.reshape(model_size, data_size, -1, gathered.shape[-1])

    def reduce_data(part_sum):
        return lax.psum_scatter(part_sum, "dp", scatter_dimension=1, tiled=True)[:, 0]

    def to_rows(part_sum):
        reduced = lax.psum_scatter(part_sum, "tp", scatter_dimension=0, tiled=True)[0]
        return lax.all_to_all(reduced, "dp", split_axis=0, concat_axis=2, tiled=True)[0]

    def local_step(x_loc, w_gate_loc, w_up_loc, w_down_loc, dy_loc):
        y_list = []
        dx_list = []
        for micro_idx in range(x_loc.shape[0]):
            x_cols = token_columns(x_loc[micro_idx])
            gate_pre = reduce_data(jnp.einsum("tkrd,df->tkrf", x_cols, w_gate_loc, preferred_element_type=jnp.float32))
            up_pre = reduce_data(jnp.einsum("tkrd,df->tkrf", x_cols, w_up_loc, preferred_element_type=jnp.float32))
            sig_gate = jax.nn.sigmoid(gate_pre)
            act_gate = gate_pre * sig_gate
            hidden = (act_gate * up_pre).astype(jnp.bfloat16)
            hidden_all = lax.all_gather(hidden, "dp", axis=1)
            out_sum = to_rows(jnp.einsum("tkrf,fd->tkrd", hidden_all, w_down_loc, preferred_element_type=jnp.float32))
            y_list.append((x_loc[micro_idx].astype(jnp.float32) + out_sum).astype(jnp.bfloat16))
            dy_cols = token_columns(dy_loc[micro_idx])
            grad_h = reduce_data(jnp.einsum("tkrd,fd->tkrf", dy_cols, w_down_loc, preferred_element_type=jnp.float32))
            grad_gate, grad_up = gate_grads(grad_h, gate_pre, up_pre, sig_gate, act_gate)
            gate_all = lax.all_gather(grad_gate, "dp", axis=1)
            up_all = lax.all_gather(grad_up, "dp", axis=1)
            dx_part = jnp.einsum("tkrf,df->tkrd", gate_all, w_gate_loc, preferred_element_type=jnp.float32) + jnp.einsum("tkrf,df->tkrd", up_all, w_up_loc, preferred_element_type=jnp.float32)
            dx_list.append((dy_loc[micro_idx].astype(jnp.float32) + to_rows(dx_part)).astype(jnp.bfloat16))
            dw_gate = jnp.einsum("tkrd,tkrf->df", x_cols, gate_all, preferred_element_type=jnp.float32)
            dw_up = jnp.einsum("tkrd,tkrf->df", x_cols, up_all, preferred_element_type=jnp.float32)
            dw_down = jnp.einsum("tkrf,tkrd->fd", hidden_all, dy_cols, preferred_element_type=jnp.float32)
            if micro_idx == 0:
                gate_sum, up_sum, down_sum = dw_gate, dw_up, dw_down
            else:
                gate_sum = gate_sum + dw_gate
                up_sum = up_sum + dw_up
                down_sum = down_sum + dw_down
        return jnp.stack(y_list), jnp.stack(dx_list), gate_sum, up_sum, down_sum

    return jax.shard_map(local_step, mesh=mesh, in_specs=in_specs, out_specs=out_specs, check_vma=False)
```

profile of v0, /device:TPU:0, one launch (start us, length us, event | category | flops | bytes accessed | tf_op | source)
XLA Modules:
  0.0 525.0 jit_solution(11277314349216603657)
XLA Ops:
  7.2 1.5 fusion.56
  8.7 5.5 %all-to-all-start.2 = ((bf16[8,8,512]{2,0,1:T(8,128)(2,1)}), bf16[8,8,512]{2,0,1:T(8,128)(2,1)S(1)}, u32[]{:S(2)}, u32[]{:S(2)}) async-start(bf16[8,8,512]{2,0,1:T(8,128)(2,1)} %bitcast.14), calls=%async_computation.3 | async-start | bytes 131072 | tf_op jit(solution)/shard_map/all_to_all | solution.py:21
  14.2 1.5 fusion.55
  15.7 3.3 all-to-all-done.2
  19.0 3.4 all-to-all-start
  22.3 5.1 all_gather.52
  27.4 5.2 fusion.14
  32.6 2.5 fusion.22
  35.1 4.0 all-to-all-start.6
  39.1 5.2 all_gather.49
  44.3 5.1 fusion.16
  49.4 4.0 all-to-all-start.4
  53.4 5.1 fusion.24
  58.5 5.1 all_gather.59
  63.6 4.9 all_gather.55
  68.5 6.1 %fusion.2 = f32[2,8,8,5504]{3,2,1,0:T(8,128)} fusion(bf16[5504,512]{1,0:T(8,128)(2,1)} %param.8, bf16[2,64,512]{2,1,0:T(8,128)(2,1)S(1)} %all_gather.59), kind=kOutput, calls=%fused_computation.5 | convolution fusion | flops 721420288 | bytes 8585216 | tf_op jit(solution)/shard_map/tkrd,fd->tkrf/dot_general | solution.py:46
  74.6 6.1 %fusion.4 = f32[2,8,8,5504]{3,2,1,0:T(8,128)} fusion(bf16[5504,512]{1,0:T(8,128)(2,1)} %param.8, bf16[2,64,512]{2,1,0:T(8,128)(2,1)S(1)} %all_gather.55), kind=kOutput, calls=%fused_computation.7 | convolution fusion | flops 721420288 | bytes 8585216 | tf_op jit(solution)/shard_map/tkrd,fd->tkrf/dot_general | solution.py:46
  80.8 0.0 all-gather.7.cloned.1.call-start
  80.8 0.6 copy-done.11
  81.4 0.6 dynamic-slice
  82.0 210.6 %all-reduce.9.cloned.1.call-done = (f32[2,8,8,5504]{3,2,1,0:T(8,128)}, f32[2,8,8,5504]{3,2,1,0:T(8,128)}, f32[2,8,8,5504]{3,2,1,0:T(8,128)}, f32[2,8,8,5504]{3,2...) async-done(((f32[2,8,8,5504]{3,2,1,0:T(8,128)}, f32[2,8,8,5504]{3,2,1,0:T(8,128)}, f32[2,8,8,5504]{3,2,1,0:T(8,128)}, f32[2,8,8,5504]{3,2,1,0:T(8,128)}, ...) | async-done | bytes 16908304
  292.6 2.8 multiply_convert_fusion.3
  295.4 0.0 all-gather.9.cloned.1.call-start
  295.5 2.8 multiply_convert_fusion.1
  298.3 0.0 all-gather.13.cloned.1.call-start
  298.3 0.5 all-gather.13.cloned.1.call-update
  298.9 0.0 all-gather.11.cloned.1.call-start
  298.9 0.5 all-gather.11.cloned.1.call-update
  299.4 0.0 all-gather.17.cloned.1.call-start
  299.5 0.5 all-gather.17.cloned.1.call-update
  300.0 0.0 all-gather.15.cloned.1.call-start
  300.1 0.7 all-gather.15.cloned.1.call-update
  300.8 0.0 reduce-scatter.11.cloned.1.call-start
  300.8 15.8 %all-gather.7.cloned.1.call-done = bf16[2,8,8,5504]{3,2,1,0:T(8,128)(2,1)} async-done(((bf16[2,1,8,5504]{3,2,1,0:T(8,128)(2,1)}), bf16[2,8,8,5504]{3,2,1,0:T(8,128)(2,1)}) %all-gather.7.cloned.1.call-update) | async-done | bytes 1409040 | tf_op jit(solution)/shard_map/all_gather | solution.py:42
  316.6 4.7 fusion.8
  321.3 0.0 reduce-scatter.13.cloned.1.call-start
  321.3 18.6 %all-gather.9.cloned.1.call-done = bf16[2,8,8,5504]{3,2,1,0:T(8,128)(2,1)} async-done(((bf16[2,1,8,5504]{3,2,1,0:T(8,128)(2,1)}), bf16[2,8,8,5504]{3,2,1,0:T(8,128)(2,1)}) %all-gather.9.cloned.1.call-update) | async-done | bytes 1409040 | tf_op jit(solution)/shard_map/all_gather | solution.py:42
  339.9 4.7 fusion.6
  344.6 0.2 reduce-scatter.15.cloned.1.call-start
  344.9 17.7 %all-gather.13.cloned.1.call-done = bf16[2,8,8,5504]{3,2,1,0:T(8,128)(2,1)} async-done(((bf16[2,1,8,5504]{3,2,1,0:T(8,128)(2,1)}), bf16[2,8,8,5504]{3,2,1,0:T(8,128)(2,1)}) %all-gather.13.cloned.1.call-update) | async-done | bytes 1409040 | tf_op jit(solution)/shard_map/all_gather | solution.py:49
  362.5 5.0 fusion.12
  367.5 18.2 %all-gather.11.cloned.1.call-done = bf16[2,8,8,5504]{3,2,1,0:T(8,128)(2,1)} async-done(((bf16[2,1,8,5504]{3,2,1,0:T(8,128)(2,1)}), bf16[2,8,8,5504]{3,2,1,0:T(8,128)(2,1)}) %all-gather.11.cloned.1.call-update) | async-done | bytes 1409040 | tf_op jit(solution)/shard_map/all_gather | solution.py:48
  385.7 5.7 %fusion.35 = f32[2,8,8,512]{3,2,1,0:T(8,128)} fusion(f32[2,8,8,512]{3,2,1,0:T(8,128)S(1)} %fusion.12, bf16[2,8,8,5504]{3,2,1,0:T(8,128)(2,1)} %all-gather.11.cloned.1.call-done, bf16[512,5504]{1,0:T(8,128)(2,1)} %param.6), kind=kOutput, calls=%fused_computation.38 | convolution fusion | flops 721485824 | bytes 7569408 | tf_op jit(solution)/shard_map/tkrf,df->tkrd/dot_general | solution.py:50
  391.5 0.0 reduce-scatter.17.cloned.1.call-start
  391.5 16.8 %all-gather.17.cloned.1.call-done = bf16[2,8,8,5504]{3,2,1,0:T(8,128)(2,1)} async-done(((bf16[2,1,8,5504]{3,2,1,0:T(8,128)(2,1)}), bf16[2,8,8,5504]{3,2,1,0:T(8,128)(2,1)}) %all-gather.17.cloned.1.call-update) | async-done | bytes 1409040 | tf_op jit(solution)/shard_map/all_gather | solution.py:49
  408.3 5.0 fusion.10
  413.3 17.8 %all-gather.15.cloned.1.call-done = bf16[2,8,8,5504]{3,2,1,0:T(8,128)(2,1)} async-done(((bf16[2,1,8,5504]{3,2,1,0:T(8,128)(2,1)}), bf16[2,8,8,5504]{3,2,1,0:T(8,128)(2,1)}) %all-gather.15.cloned.1.call-update) | async-done | bytes 1409040 | tf_op jit(solution)/shard_map/all_gather | solution.py:48
  431.1 5.7 %fusion.38 = f32[2,8,8,512]{3,2,1,0:T(8,128)} fusion(f32[2,8,8,512]{3,2,1,0:T(8,128)S(1)} %fusion.10, bf16[2,8,8,5504]{3,2,1,0:T(8,128)(2,1)} %all-gather.15.cloned.1.call-done, bf16[512,5504]{1,0:T(8,128)(2,1)} %param.6), kind=kOutput, calls=%fused_computation.39 | convolution fusion | flops 721485824 | bytes 7569408 | tf_op jit(solution)/shard_map/tkrf,df->tkrd/dot_general | solution.py:50
  436.8 1.7 fusion.33
  438.5 1.7 fusion.30
  440.2 6.0 %fusion.1 = f32[512,5504]{0,1:T(8,128)} fusion(f32[5504,512,1,1]{1,0,3,2:T(8,128)S(1)} %fusion.33, bf16[2,8,8,5504]{3,2,1,0:T(8,128)(2,1)S(1)} %copy-done.4, bf16[2,64,512]{2,1,0:T(8,128)(2,1)S(1)} %all_gather.52), kind=kOutput, calls=%fused_computation.4 | convolution fusion | flops 724238336 | bytes 24084480 | tf_op jit(solution)/shard_map/tkrd,tkrf->df/dot_general | solution.py:52
  446.3 5.9 %fusion = f32[512,5504]{0,1:T(8,128)} fusion(f32[5504,512,1,1]{1,0,3,2:T(8,128)S(1)} %fusion.30, bf16[2,8,8,5504]{3,2,1,0:T(8,128)(2,1)S(1)} %copy-done.3, bf16[2,64,512]{2,1,0:T(8,128)(2,1)S(1)} %all_gather.52), kind=kOutput, calls=%fused_computation.2 | convolution fusion | flops 724238336 | bytes 24084480 | tf_op jit(solution)/shard_map/tkrd,tkrf->df/dot_general | solution.py:53
  452.2 3.6 all-to-all-start.1
  455.8 6.0 %fusion.27 = f32[5504,512,1,1]{1,0,3,2:T(8,128)} fusion(bf16[2,8,8,5504]{3,2,1,0:T(8,128)(2,1)S(1)} %copy-done.5, bf16[2,64,512]{2,1,0:T(8,128)(2,1)S(1)} %all_gather.55), kind=kOutput, calls=%fused_computation.30 | convolution fusion | flops 721420288 | bytes 12812288 | tf_op jit(solution)/shard_map/tkrf,tkrd->fd/dot_general | solution.py:54
  461.8 3.9 all-to-all-start.3
  465.7 10.2 %bitcast_add_fusion = f32[5504,512]{1,0:T(8,128)} fusion(f32[5504,512,1,1]{1,0,3,2:T(8,128)} %fusion.27, bf16[2,8,8,5504]{3,2,1,0:T(8,128)(2,1)S(1)} %copy-done.6, bf16[2,64,512]{2,1,0:T(8,128)(2,1)S(1)} %copy-done.8), kind=kOutput, calls=%fused_computation | convolution fusion | flops 724238336 | bytes 24084480 | tf_op jit(solution)/shard_map/tkrf,tkrd->fd/dot_general | solution.py:54
  475.9 11.8 %copy.36 = f32[512,5504]{1,0:T(8,128)} copy(f32[512,5504]{0,1:T(8,128)} %fusion.1) | data formatting | bytes 22544384
  487.8 11.9 %copy.37 = f32[512,5504]{1,0:T(8,128)} copy(f32[512,5504]{0,1:T(8,128)} %fusion) | data formatting | bytes 22544384
  499.7 4.2 all-to-all-start.5
  503.9 5.2 all-to-all-done.5
  509.2 3.4 all-to-all-start.7
  512.5 0.7 pad_maximum_fusion
  513.2 4.6 all-to-all-done.7
  517.8 0.7 pad_maximum_fusion.1
  (42 shorter events, 0.3 us)
Async XLA Ops:
  8.7 10.3 %all-to-all-start.2 = ((bf16[8,8,512]{2,0,1:T(8,128)(2,1)}), bf16[8,8,512]{2,0,1:T(8,128)(2,1)S(1)}, u32[]{:S(2)}, u32[]{:S(2)}) async-start(bf16[8,8,512]{2,0,1:T(8,128)(2,1)} %bitcast.14), calls=%async_computation.3 | async-start | bytes 131072 | tf_op jit(solution)/shard_map/all_to_all | solution.py:21
  19.0 16.2 %all-to-all-start = ((bf16[8,8,512]{2,0,1:T(8,128)(2,1)}), bf16[8,8,512]{2,0,1:T(8,128)(2,1)S(1)}, u32[]{:S(2)}, u32[]{:S(2)}) async-start(bf16[8,8,512]{2,0,1:T(8,128)(2,1)} %bitcast), calls=%async_computation | async-start | bytes 131072 | tf_op jit(solution)/shard_map/all_to_all | solution.py:21
  27.4 5.2 copy-start
  35.1 14.2 %all-to-all-start.6 = ((bf16[8,8,512]{2,0,1:T(8,128)(2,1)}), bf16[8,8,512]{2,0,1:T(8,128)(2,1)S(1)}, u32[]{:S(2)}, u32[]{:S(2)}) async-start(bf16[8,8,512]{2,0,1:T(8,128)(2,1)} %bitcast.33), calls=%async_computation.9 | async-start | bytes 131072 | tf_op jit(solution)/shard_map/all_to_all | solution.py:21
  49.4 14.2 %all-to-all-start.4 = ((bf16[8,8,512]{2,0,1:T(8,128)(2,1)}), bf16[8,8,512]{2,0,1:T(8,128)(2,1)S(1)}, u32[]{:S(2)}, u32[]{:S(2)}) async-start(bf16[8,8,512]{2,0,1:T(8,128)(2,1)} %bitcast.25), calls=%async_computation.6 | async-start | bytes 131072 | tf_op jit(solution)/shard_map/all_to_all | solution.py:21
  53.3 239.3 %all-reduce.9.cloned.1.call-start = ((), (), s32[]{:S(2)}) async-start(), calls=%async_computation.22 | async-start | bytes 33816576
  63.6 11.0 %copy-start.7 = (bf16[2,64,512]{2,1,0:T(8,128)(2,1)}, bf16[2,64,512]{2,1,0:T(8,128)(2,1)S(1)}, u32[]{:S(2)}) copy-start(bf16[2,64,512]{2,1,0:T(8,128)(2,1)S(1)} %all_gather.59) | copy-start | bytes 393220
  80.7 0.7 copy-start.11
  80.8 235.8 %all-gather.7.cloned.1.call-start = ((), (), s32[]{:S(2)}) async-start(), calls=%async_computation.12 | async-start | bytes 1585152 | tf_op jit(solution)/shard_map/all_gather | solution.py:42
  295.4 44.5 %all-gather.9.cloned.1.call-start = ((), (), s32[]{:S(2)}) async-start(), calls=%async_computation.14 | async-start | bytes 1585152 | tf_op jit(solution)/shard_map/all_gather | solution.py:42
  298.3 64.3 %all-gather.13.cloned.1.call-start = ((), (), s32[]{:S(2)}) async-start(), calls=%async_computation.17 | async-start | bytes 1585152 | tf_op jit(solution)/shard_map/all_gather | solution.py:49
  298.9 86.9 %all-gather.11.cloned.1.call-start = ((), (), s32[]{:S(2)}) async-start(), calls=%async_computation.16 | async-start | bytes 1585152 | tf_op jit(solution)/shard_map/all_gather | solution.py:48
  299.4 108.9 %all-gather.17.cloned.1.call-start = ((), (), s32[]{:S(2)}) async-start(), calls=%async_computation.20 | async-start | bytes 1585152 | tf_op jit(solution)/shard_map/all_gather | solution.py:49
  300.0 131.1 %all-gather.15.cloned.1.call-start = ((), (), s32[]{:S(2)}) async-start(), calls=%async_computation.19 | async-start | bytes 1585152 | tf_op jit(solution)/shard_map/all_gather | solution.py:48
  300.8 151.4 %reduce-scatter.11.cloned.1.call-start = ((), (), s32[]{:S(2)}) async-start(), calls=%async_computation.13 | async-start | bytes 393216 | tf_op jit(solution)/shard_map/reduce_scatter | solution.py:29
  321.3 140.5 %reduce-scatter.13.cloned.1.call-start = ((), (), s32[]{:S(2)}) async-start(), calls=%async_computation.15 | async-start | bytes 393216 | tf_op jit(solution)/shard_map/reduce_scatter | solution.py:29
  344.6 155.0 %reduce-scatter.15.cloned.1.call-start = ((), (), s32[]{:S(2)}) async-start(), calls=%async_computation.18 | async-start | bytes 393216 | tf_op jit(solution)/shard_map/reduce_scatter | solution.py:29
  391.5 112.5 %reduce-scatter.17.cloned.1.call-start = ((), (), s32[]{:S(2)}) async-start(), calls=%async_computation.21 | async-start | bytes 393216 | tf_op jit(solution)/shard_map/reduce_scatter | solution.py:29
  413.3 23.5 %copy-start.2 = (bf16[2,8,8,5504]{3,2,1,0:T(8,128)(2,1)S(1)}, bf16[2,8,8,5504]{3,2,1,0:T(8,128)(2,1)}, u32[]{:S(2)}) copy-start(bf16[2,8,8,5504]{3,2,1,0:T(8,128)(2,1)} %all-gather.11.cloned.1.call-done) | copy-start | bytes 4227076
  436.8 1.7 copy-start.1
  438.5 1.7 copy-start.4
  440.2 6.0 %copy-start.3 = (bf16[2,8,8,5504]{3,2,1,0:T(8,128)(2,1)S(1)}, bf16[2,8,8,5504]{3,2,1,0:T(8,128)(2,1)}, u32[]{:S(2)}) copy-start(bf16[2,8,8,5504]{3,2,1,0:T(8,128)(2,1)} %all-gather.17.cloned.1.call-done) | copy-start | bytes 4227076
  446.3 9.5 %copy-start.5 = (bf16[2,8,8,5504]{3,2,1,0:T(8,128)(2,1)S(1)}, bf16[2,8,8,5504]{3,2,1,0:T(8,128)(2,1)}, u32[]{:S(2)}) copy-start(bf16[2,8,8,5504]{3,2,1,0:T(8,128)(2,1)} %all-gather.7.cloned.1.call-done) | copy-start | bytes 4227076
  452.2 9.7 %all-to-all-start.1 = ((f32[8,8,512]{2,1,0:T(8,128)}), f32[8,8,512]{2,1,0:T(8,128)S(1)}, u32[]{:S(2)}, u32[]{:S(2)}) async-start(f32[8,8,512]{2,1,0:T(8,128)} %bitcast.172), calls=%async_computation.2 | async-start | bytes 262144 | tf_op jit(solution)/shard_map/all_to_all | solution.py:30
  455.8 9.9 %copy-start.6 = (bf16[2,8,8,5504]{3,2,1,0:T(8,128)(2,1)S(1)}, bf16[2,8,8,5504]{3,2,1,0:T(8,128)(2,1)}, u32[]{:S(2)}) copy-start(bf16[2,8,8,5504]{3,2,1,0:T(8,128)(2,1)} %all-gather.9.cloned.1.call-done) | copy-start | bytes 4227076
  455.8 9.9 %copy-start.8 = (bf16[2,64,512]{2,1,0:T(8,128)(2,1)S(1)}, bf16[2,64,512]{2,1,0:T(8,128)(2,1)}, u32[]{:S(2)}) copy-start(bf16[2,64,512]{2,1,0:T(8,128)(2,1)} %copy-done.7) | copy-start | bytes 393220
  461.8 37.9 %all-to-all-start.3 = ((f32[8,8,512]{2,1,0:T(8,128)}), f32[8,8,512]{2,1,0:T(8,128)S(1)}, u32[]{:S(2)}, u32[]{:S(2)}) async-start(f32[8,8,512]{2,1,0:T(8,128)} %bitcast.170), calls=%async_computation.5 | async-start | bytes 262144 | tf_op jit(solution)/shard_map/all_to_all | solution.py:30
  487.8 16.1 %copy-start.9 = (bf16[2,8,4096]{2,1,0:T(8,128)(2,1)S(1)}, bf16[2,8,4096]{2,1,0:T(8,128)(2,1)}, u32[]{:S(2)}) copy-start(bf16[2,8,4096]{2,1,0:T(8,128)(2,1)} %param.5) | copy-start | bytes 393220
  487.8 30.0 %copy-start.10 = (bf16[2,8,4096]{2,1,0:T(8,128)(2,1)S(1)}, bf16[2,8,4096]{2,1,0:T(8,128)(2,1)}, u32[]{:S(2)}) copy-start(bf16[2,8,4096]{2,1,0:T(8,128)(2,1)} %param.9) | copy-start | bytes 393220
  499.7 9.5 %all-to-all-start.5 = ((f32[8,8,512]{2,1,0:T(8,128)}), f32[8,8,512]{2,1,0:T(8,128)S(1)}, u32[]{:S(2)}, u32[]{:S(2)}) async-start(f32[8,8,512]{2,1,0:T(8,128)} %bitcast.171), calls=%async_computation.8 | async-start | bytes 262144 | tf_op jit(solution)/shard_map/all_to_all | solution.py:30
  509.2 8.6 %all-to-all-start.7 = ((f32[8,8,512]{2,1,0:T(8,128)}), f32[8,8,512]{2,1,0:T(8,128)S(1)}, u32[]{:S(2)}, u32[]{:S(2)}) async-start(f32[8,8,512]{2,1,0:T(8,128)} %bitcast.173), calls=%async_computation.11 | async-start | bytes 262144 | tf_op jit(solution)/shard_map/all_to_all | solution.py:30
Sparse Core Ops, SparseCore 0:
  80.9 211.6 all-reduce.8
  295.5 20.9 all-gather.6
  319.0 20.8 all-gather.8
  341.6 20.8 all-gather.12
  364.8 20.8 all-gather.10
  387.4 20.8 all-gather.16
  410.2 20.8 all-gather.14
  433.9 9.7 reduce-scatter.10
  446.5 9.7 reduce-scatter.12
  458.4 9.7 reduce-scatter.14
  470.4 9.7 reduce-scatter.16
where the time goes:
time: 527 us; the launch traced here: 525 us
  waiting for transfers between devices  331 us (63%)
  matrix products  92.3 us (18%)
  starting transfers between devices  32.4 us (6%)
  local copies, waits for them, and re-layouts  28 us (5%)
  blocking collectives  20.2 us (4%)
  between operations  14.1 us (3%)
  other arithmetic  6.94 us (1%)
    unnamed x12, waiting for transfers between devices  213 us
    all_gather x2, waiting for transfers between devices, local_step(): gate_all = lax.all_gather(grad_gate, 'dp', axis=1)  35.9 us
    all_gather x2, waiting for transfers between devices, local_step(): up_all = lax.all_gather(grad_up, 'dp', axis=1)  34.5 us
    all_gather x2, waiting for transfers between devices, local_step(): hidden_all = lax.all_gather(hidden, 'dp', axis=1)  34.4 us
    unnamed x27, local copies, waits for them, and re-layouts  24.9 us
    all_gather x4, blocking collectives, token_columns(): gathered = lax.all_gather(spread, 'tp', axis=0)  20.2 us
    all_to_all x4, starting transfers between devices, token_columns(): lax.all_to_all(rows_loc, 'dp', split_axis=1, concat_axis=0, tiled=True)  16.8 us
    dot_general x2, matrix products, local_step(): jnp.einsum('tkrf,tkrd->fd', hidden_all, dy_cols, preferred_element_type=j...  16.2 us
  transfers between devices with their start and end apart: 19, of which 10 were waited for; matrix products, arithmetic and copies ran while one was open for 21% of the time, Pallas kernels for 0%

commit v1 on v0

v1 whole, which is shorter than its diff:
```python
import functools

import jax
import jax.numpy as jnp
from jax import lax
from jax.experimental import pallas as pl
from jax.experimental.pallas import tpu as pltpu
from jax.sharding import PartitionSpec as P

MESH = pl.DeviceIdType.MESH
LANES = 128
SLOTS = 8
LAGS = (1, 2, 2, 2, 2, 1)
STARTS = tuple(sum(LAGS[:k]) for k in range(len(LAGS) + 1))
TRANS_B = (((1,), (1,)), ((), ()))
TRANS_A = (((0,), (0,)), ((), ()))


def dot_f32(lhs, rhs):
    return jnp.dot(lhs, rhs, preferred_element_type=jnp.float32)


def dot_t(lhs, rhs):
    return lax.dot_general(lhs, rhs, TRANS_B, preferred_element_type=jnp.float32)


def exchange_kernel(tiles, x_hbm, dy_hbm, wg_hbm, wu_hbm, wd_hbm,
                    act_hbm, tok_hbm, out_hbm,
                    loc, tok, rows, wg, wu, wd, part, core_in, first_out, first_in, second_out, second_in, act, acc,
                    load_sem, tok_send, tok_recv, send_sem, recv_sem, store_sem):
    tp = lax.axis_index("tp")
    dp = lax.axis_index("dp")
    core = lax.rem(dp, 2)
    xpos = lax.rem(lax.div(dp, 2), 2)
    ypos = lax.div(dp, 4)
    me = dp * 2 + tp

    def device(fc, fx, fy, fz):
        dc = 1 - core if fc else core
        dx = 1 - xpos if fx else xpos
        dy = 1 - ypos if fy else ypos
        return (1 - tp if fz else tp, dy * 4 + dx * 2 + dc)

    core_peer = device(1, 0, 0, 0)
    x_peer = device(0, 1, 0, 0)
    y_peer = device(0, 0, 1, 0)

    token_loads = [pltpu.make_async_copy(x_hbm, loc.at[0], load_sem.at[0]),
                   pltpu.make_async_copy(dy_hbm, loc.at[1], load_sem.at[1])]
    weight_loads = [pltpu.make_async_copy(wg_hbm, wg, load_sem.at[2]),
                    pltpu.make_async_copy(wu_hbm, wu, load_sem.at[3]),
                    pltpu.make_async_copy(wd_hbm, wd, load_sem.at[4])]
    for cp in token_loads + weight_loads:
        cp.start()

    others = [((k >> 0) & 1, (k >> 1) & 1, (k >> 2) & 1, (k >> 3) & 1) for k in range(1, 16)]
    barrier = pltpu.get_barrier_semaphore()
    for flags in others:
        pl.semaphore_signal(barrier, 1, device_id=device(*flags), device_id_type=MESH)
    for cp in token_loads:
        cp.wait()
    pl.semaphore_wait(barrier, 15)

    for mb in range(2):
        for arr in range(2):
            for flags in others:
                dest = device(*flags)
                pltpu.make_async_remote_copy(
                    src_ref=loc.at[arr, mb, :, pl.ds(pl.multiple_of(dest[1] * 512, 512), 512)],
                    dst_ref=tok.at[arr, mb, me],
                    send_sem=tok_send.at[arr, mb], recv_sem=tok_recv.at[arr, mb],
                    device_id=dest, device_id_type=MESH).start()
    for mb in range(2):
        for arr in range(2):
            tok[arr, mb, me] = loc[arr, mb, :, pl.ds(pl.multiple_of(dp * 512, 512), 512)]

    def tokens_in(arr, mb):
        part15 = tok.at[arr, mb, pl.ds(0, 15)]
        pltpu.make_async_copy(part15, part15, tok_recv.at[arr, mb]).wait()
        for pair in range(8):
            lo = tok[arr, mb, 2 * pair].astype(jnp.float32)
            hi = tok[arr, mb, 2 * pair + 1].astype(jnp.float32)
            rows[arr, pl.ds(mb * 128 + 16 * pair, 16), :] = jnp.concatenate([lo, hi], axis=0).astype(jnp.bfloat16)

    acc[...] = jnp.zeros_like(acc)
    tokens_in(0, 0)
    tokens_in(1, 0)
    for cp in weight_loads:
        cp.wait()

    n_iter = tiles

    def unit(i, h):
        u = 2 * i + h
        mb = lax.div(u, tiles)
        return u, mb, u - tiles * mb

    keep_core = pl.multiple_of(core * 64, 64)
    send_core = pl.multiple_of((1 - core) * 64, 64)
    pos1 = (xpos, ypos)
    pos2 = (ypos, xpos)
    peer1 = (x_peer, y_peer)
    peer2 = (y_peer, x_peer)

    def off(v):
        return pl.multiple_of(v, 16)

    def copies(stage, i, h):
        u, mb, t = unit(i, h)
        slot = lax.rem(i, SLOTS)
        base = mb * 128 + core * 64
        if stage == 0:
            src, dst, dev = part.at[slot, h, :, pl.ds(send_core, 64), :], core_in.at[u], core_peer
        elif stage == 1:
            src, dst, dev = first_out.at[slot, h], first_in.at[u], peer1[h]
        elif stage == 2:
            src, dst, dev = second_out.at[slot, h], second_in.at[u], peer2[h]
        elif stage == 3:
            src = dst = act.at[t, :, pl.ds(off(base + 32 * pos1[h] + 16 * pos2[h]), 16), :]
            dev = peer2[h]
        elif stage == 4:
            src = dst = act.at[t, :, pl.ds(off(base + 32 * pos1[h]), 32), :]
            dev = peer1[h]
        else:
            src = dst = act.at[t, :, pl.ds(off(base), 64), :]
            dev = core_peer
        return pltpu.make_async_remote_copy(
            src_ref=src, dst_ref=dst, send_sem=send_sem.at[stage, h, slot], recv_sem=recv_sem.at[stage, h, slot],
            device_id=dev, device_id_type=MESH)

    def stage_partials(i):
        for h in range(2):
            u, mb, t = unit(i, h)
            slot = lax.rem(i, SLOTS)
            cols = pl.ds(pl.multiple_of(t * LANES, LANES), LANES)
            r = pl.ds(pl.multiple_of(mb * 128, 128), 128)
            pair = jnp.concatenate([wg[:, cols], wu[:, cols]], axis=1)
            ab = dot_f32(rows[0, r, :], pair)
            part[slot, h, 0] = ab[:, :LANES]
            part[slot, h, 1] = ab[:, LANES:]
            part[slot, h, 2] = dot_t(rows[1, r, :], wd[cols, :])
            copies(0, i, h).start()

    def stage_first(i):
        slot = lax.rem(i, SLOTS)
        for h in range(2):
            u, _, _ = unit(i, h)
            copies(0, i, h).wait()
            o = (1 - pos1[h]) * 32
            first_out[slot, h] = (part[slot, h, :, pl.ds(off(core * 64 + o), 32), :] + core_in[u, :, pl.ds(off(o), 32), :])
            copies(1, i, h).start()

    def stage_second(i):
        slot = lax.rem(i, SLOTS)
        for h in range(2):
            u, _, _ = unit(i, h)
            copies(1, i, h).wait()
            o2 = (1 - pos2[h]) * 16
            o = pos1[h] * 32 + o2
            second_out[slot, h] = (part[slot, h, :, pl.ds(off(core * 64 + o), 16), :] + core_in[u, :, pl.ds(off(o), 16), :]
                                   + first_in[u, :, pl.ds(off(o2), 16), :])
            copies(2, i, h).start()

    def stage_act(i):
        slot = lax.rem(i, SLOTS)
        for h in range(2):
            u, mb, t = unit(i, h)
            copies(2, i, h).wait()
            o2 = pos2[h] * 16
            o = pos1[h] * 32 + o2
            tot = (part[slot, h, :, pl.ds(off(core * 64 + o), 16), :] + core_in[u, :, pl.ds(off(o), 16), :]
                   + first_in[u, :, pl.ds(off(o2), 16), :] + second_in[u])
            a, b, g = tot[0], tot[1], tot[2]
            s = jax.nn.sigmoid(a)
            silu = a * s
            r = pl.ds(off(mb * 128 + core * 64 + o), 16)
            act[t, 0, r, :] = (silu * b).astype(jnp.bfloat16)
            act[t, 1, r, :] = (g * b * s * (1.0 + a * (1.0 - s))).astype(jnp.bfloat16)
            act[t, 2, r, :] = (g * silu).astype(jnp.bfloat16)
            copies(3, i, h).start()

    def stage_forward(stage, i):
        for h in range(2):
            copies(stage - 1, i, h).wait()
            copies(stage, i, h).start()

    def stage_outputs(i):
        for h in range(2):
            u, mb, t = unit(i, h)
            copies(5, i, h).wait()
            cols = pl.ds(pl.multiple_of(t * LANES, LANES), LANES)
            r = pl.ds(pl.multiple_of(mb * 128, 128), 128)
            acc[0, r, :] += dot_f32(act[t, 0, r, :], wd[cols, :])
            grads = jnp.concatenate([act[t, 1, r, :], act[t, 2, r, :]], axis=1)
            pair = jnp.concatenate([wg[:, cols], wu[:, cols]], axis=1)
            acc[1, r, :] += dot_t(grads, pair)

            pltpu.make_async_copy(act.at[t, :, r, :], act_hbm.at[t, :, r, :], store_sem.at[0]).start()

    def body(j, carry):
        def run(stage, fn):
            i = j - STARTS[stage]
            pl.when(jnp.logical_and(i >= 0, i < n_iter))(functools.partial(fn, i))

        run(5, functools.partial(stage_forward, 5))
        run(4, functools.partial(stage_forward, 4))
        run(3, stage_act)
        run(2, stage_second)
        run(1, stage_first)

        @pl.when(j == tiles // 2 - 2)
        def _():
            tokens_in(0, 1)
            tokens_in(1, 1)
            pltpu.make_async_copy(rows, tok_hbm, store_sem.at[1]).start()

        run(0, stage_partials)
        run(6, stage_outputs)
        return carry

    lax.fori_loop(0, n_iter + STARTS[6], body, 0)

    out_copy = pltpu.make_async_copy(acc, out_hbm, store_sem.at[2])
    out_copy.start()
    for mb in range(2):
        for arr in range(2):
            part15 = tok.at[arr, mb, pl.ds(0, 15)]
            pltpu.make_async_copy(part15, part15, tok_send.at[arr, mb]).wait()
    pltpu.make_async_copy(rows, tok_hbm, store_sem.at[1]).wait()
    pltpu.make_async_copy(act, act_hbm, store_sem.at[0]).wait()
    out_copy.wait()


def exchange(x_loc, dy_loc, w_gate, w_up, w_down):
    d_loc, f_loc = w_gate.shape
    tiles = f_loc // LANES
    any_spec = pl.BlockSpec(memory_space=pl.ANY)
    f32, bf16 = jnp.float32, jnp.bfloat16
    return pl.pallas_call(
        functools.partial(exchange_kernel, tiles),
        out_shape=(jax.ShapeDtypeStruct((tiles, 3, 256, LANES), bf16),
                   jax.ShapeDtypeStruct((2, 256, d_loc), bf16),
                   jax.ShapeDtypeStruct((2, 256, d_loc), f32)),
        in_specs=[any_spec] * 5,
        out_specs=(any_spec, any_spec, any_spec),
        scratch_shapes=[
            pltpu.VMEM((2, 2, 8, 4096), bf16),
            pltpu.VMEM((2, 2, 16, 8, d_loc), bf16),
            pltpu.VMEM((2, 256, d_loc), bf16),
            pltpu.VMEM((d_loc, f_loc), bf16),
            pltpu.VMEM((d_loc, f_loc), bf16),
            pltpu.VMEM((f_loc, d_loc), bf16),
            pltpu.VMEM((SLOTS, 2, 3, 128, LANES), f32),
            pltpu.VMEM((2 * tiles, 3, 64, LANES), f32),
            pltpu.VMEM((SLOTS, 2, 3, 32, LANES), f32),
            pltpu.VMEM((2 * tiles, 3, 32, LANES), f32),
            pltpu.VMEM((SLOTS, 2, 3, 16, LANES), f32),
            pltpu.VMEM((2 * tiles, 3, 16, LANES), f32),
            pltpu.VMEM((tiles, 3, 256, LANES), bf16),
            pltpu.VMEM((2, 256, d_loc), f32),
            pltpu.SemaphoreType.DMA((5,)),
            pltpu.SemaphoreType.DMA((2, 2)),
            pltpu.SemaphoreType.DMA((2, 2)),
            pltpu.SemaphoreType.DMA((6, 2, SLOTS)),
            pltpu.SemaphoreType.DMA((6, 2, SLOTS)),
            pltpu.SemaphoreType.DMA((3,)),
        ],
        compiler_params=pltpu.CompilerParams(collective_id=0, has_side_effects=True, vmem_limit_bytes=60 * 2**20),
        cost_estimate=pl.CostEstimate(flops=9 * 10**9, bytes_accessed=28 * 10**6, transcendentals=0),
        name="exchange",
    )(x_loc, dy_loc, w_gate, w_up, w_down)


GROUP = 4


def gate_up_kernel(tok_ref, act_ref, dg_ref, du_ref, xt_ref):
    @pl.when(pl.program_id(0) == 0)
    def _():
        xt_ref[...] = tok_ref[0].T

    for k in range(GROUP):
        dg_ref[:, k * LANES:(k + 1) * LANES] = dot_f32(xt_ref[...], act_ref[k, 1])
        du_ref[:, k * LANES:(k + 1) * LANES] = dot_f32(xt_ref[...], act_ref[k, 2])


def down_kernel(tok_ref, act_ref, dd_ref):
    for k in range(GROUP):
        dd_ref[k * LANES:(k + 1) * LANES, :] = lax.dot_general(
            act_ref[k, 0], tok_ref[1], TRANS_A, preferred_element_type=jnp.float32)


def weight_grads(tok, act):
    tiles = act.shape[0]
    d_loc = tok.shape[-1]
    f_loc = tiles * LANES
    grid = (pl.cdiv(tiles, GROUP),)
    tok_spec = pl.BlockSpec((2, 256, d_loc), lambda i: (0, 0, 0))
    act_spec = pl.BlockSpec((GROUP, 3, 256, LANES), lambda i: (i, 0, 0, 0))
    flops = 2 * 256 * d_loc * f_loc
    width = GROUP * LANES
    dg, du = pl.pallas_call(
        gate_up_kernel, grid=grid, in_specs=[tok_spec, act_spec],
        out_specs=[pl.BlockSpec((d_loc, width), lambda i: (0, i))] * 2,
        out_shape=[jax.ShapeDtypeStruct((d_loc, f_loc), jnp.float32)] * 2,
        scratch_shapes=[pltpu.VMEM((d_loc, 256), jnp.bfloat16)],
        cost_estimate=pl.CostEstimate(flops=2 * flops, bytes_accessed=31 * 10**6, transcendentals=0),
        name="gate_up_grads",
    )(tok, act)
    dd = pl.pallas_call(
        down_kernel, grid=grid, in_specs=[tok_spec, act_spec],
        out_specs=pl.BlockSpec((width, d_loc), lambda i: (i, 0)),
        out_shape=jax.ShapeDtypeStruct((f_loc, d_loc), jnp.float32),
        cost_estimate=pl.CostEstimate(flops=flops, bytes_accessed=16 * 10**6, transcendentals=0),
        name="down_grads",
    )(tok, act)
    return dg, du, dd


def solution(mesh):
    row_spec = P(None, ("dp", "tp"), None)
    in_specs = (row_spec, P("dp", "tp"), P("dp", "tp"), P("tp", "dp"), row_spec)
    out_specs = (row_spec, row_spec, P("dp", "tp"), P("dp", "tp"), P("tp", "dp"))

    def local_step(x_loc, w_gate, w_up, w_down, dy_loc):
        act, tok, part = exchange(x_loc, dy_loc, w_gate, w_up, w_down)
        tp = lax.axis_index("tp")
        part = part.reshape(2, 2, 8, 2, 8, 512)
        keep = lax.dynamic_index_in_dim(part, tp, axis=3, keepdims=False)
        send = lax.dynamic_index_in_dim(part, 1 - tp, axis=3, keepdims=False)
        recv = lax.ppermute(send, "tp", [(0, 1), (1, 0)])
        base = lax.dynamic_index_in_dim(tok.reshape(2, 2, 8, 2, 8, 512), tp, axis=3, keepdims=False)
        out = (base.astype(jnp.float32) + (keep + recv)).astype(jnp.bfloat16)
        out = lax.all_to_all(out, "dp", split_axis=2, concat_axis=4, tiled=True)
        out = out.reshape(2, 2, 8, 4096)
        dg, du, dd = weight_grads(tok, act)
        return out[0], out[1], dg, du, dd

    return jax.shard_map(local_step, mesh=mesh, in_specs=in_specs, out_specs=out_specs, check_vma=False)
```

time: 527 us -> 165 us (0.31)
  waiting for transfers between devices: 331 us -> 0.01 us
  Pallas kernels: 0 us -> 154 us
  matrix products: 92.3 us -> 0 us
  starting transfers between devices: 32.4 us -> 4.96 us
  local copies, waits for them, and re-layouts: 28 us -> 2.95 us
  blocking collectives: 20.2 us -> 0 us
  between operations: 14.1 us -> 0.69 us
  other arithmetic: 6.94 us -> 0.87 us
    unnamed x12 -> x0, waiting for transfers between devices: 213 us -> none
    pallas_call x0 -> x3, Pallas kernels: none -> 154 us  [the longest x1 126 us: exchange(): pl.pallas_call(functools.partial(exchange_kernel, tiles), out_shape=(jax....]
    all_gather x6 -> x0, waiting for transfers between devices: 105 us -> none  [the longest x2 35.9 us: local_step(): gate_all = lax.all_gather(grad_gate, 'dp', axis=1)]
    dot_general x18 -> x0, matrix products: 92.3 us -> none  [the longest x2 16.2 us: local_step(): jnp.einsum('tkrf,tkrd->fd', hidden_all, dy_cols, preferred_element_type=j...]
    all_to_all x8 -> x1, starting transfers between devices: 31.8 us -> 3.41 us  [local_step(): out = lax.all_to_all(out, 'dp', split_axis=2, concat_axis=4, tiled=True)]
    unnamed x27 -> x2, local copies, waits for them, and re-layouts: 24.9 us -> 0.01 us
    all_gather x4 -> x0, blocking collectives: 20.2 us -> none  [token_columns(): gathered = lax.all_gather(spread, 'tp', axis=0)]
    all_to_all x8 -> x1, waiting for transfers between devices: 13.1 us -> 0.01 us  [local_step(): out = lax.all_to_all(out, 'dp', split_axis=2, concat_axis=4, tiled=True)]
  transfers between devices with their start and end apart: 19 -> 2, of which waited for: 10 -> 0; matrix products, arithmetic and copies ran while one was open for 21% -> 0% of each run, Pallas kernels for 0% -> 17%
where the time goes in v1:
time: 165 us; the launch traced here: 164 us
  Pallas kernels  154 us (93%)
  starting transfers between devices  4.96 us (3%)
  local copies, waits for them, and re-layouts  2.95 us (2%)
    pallas_call x1, Pallas kernels, exchange(): pl.pallas_call(functools.partial(exchange_kernel, tiles), out_shape=(jax....  126 us
    pallas_call x1, Pallas kernels, weight_grads(): pl.pallas_call(gate_up_kernel, grid=grid, in_specs=[tok_spec, act_spec],...  15.5 us
    pallas_call x1, Pallas kernels, weight_grads(): pl.pallas_call(down_kernel, grid=grid, in_specs=[tok_spec, act_spec], out...  12.8 us
    all_to_all x1, starting transfers between devices, local_step(): out = lax.all_to_all(out, 'dp', split_axis=2, concat_axis=4, tiled=True)  3.41 us
  transfers between devices with their start and end apart: 2, of which 0 were waited for; matrix products, arithmetic and copies ran while one was open for 0% of the time, Pallas kernels for 17%

profile of v1, /device:TPU:0, one launch (start us, length us, event | category | flops | bytes accessed | tf_op | source)
XLA Modules:
  0.0 163.7 jit_solution(5431331339829752638)
XLA Ops:
  0.6 125.8 %exchange.1 = (bf16[43,3,256,128]{3,2,1,0:T(8,128)(2,1)}, bf16[2,256,512]{2,1,0:T(8,128)(2,1)}, f32[2,256,512]{2,1,0:T(8,128)}) custom-call(bf16[2,8,4096]{2,1,0:T(8,128)(2,1)} %x_hbm.1, bf16[2,8,4096]{2,1,0:T(8,128)(2,1)} %dy_hbm.1, bf16[512,5504]{1,0:T(8,128)(2,1)} %wg_hbm.1, bf16[512,5504]{1,0:T(8,128)(2,1)} %wu_hbm.1, bf16[5504,512]{1,0:T(8,128)(2,1)} %wd_hbm.1), custom_call_target="tpu_custom_call" | custom-call | flops 8999999488 | bytes 28000000 | tf_op jit(solution)/shard_map/exchange/pallas_call | solution.py:239
  126.5 1.3 constant_dynamic-slice_fusion.1
  127.8 1.6 collective-permute-start
  129.4 0.0 copy-start
  129.4 12.8 %down_grads.1 = f32[5504,512]{1,0:T(8,128)} custom-call(bf16[2,256,512]{2,1,0:T(8,128)(2,1)} %get-tuple-element.10.tok_ref, bf16[43,3,256,128]{3,2,1,0:T(8,128)(2,1)} %get-tuple-element.12.act_ref), custom_call_target="tpu_custom_call" | custom-call | flops 1442840576 | bytes 16000000 | tf_op jit(solution)/shard_map/down_grads/pallas_call | solution.py:310
  142.2 0.0 collective-permute-done
  142.2 0.0 copy-done
  142.2 0.9 fusion
  143.1 3.4 %all-to-all-start = ((bf16[2,2,8,8,512]{4,3,1,0,2:T(8,128)(2,1)}), bf16[2,2,8,8,512]{4,3,1,0,2:T(8,128)(2,1)S(1)}, u32[]{:S(2)}, u32[]{:S(2)}) async-start(bf16[2,2,8,8,512]{4,3,1,0,2:T(8,128)(2,1)} %fusion), calls=%async_computation | async-start | bytes 524288 | tf_op jit(solution)/shard_map/all_to_all | solution.py:334
  146.5 15.5 %gate_up_grads.1 = (f32[512,5504]{1,0:T(8,128)}, f32[512,5504]{1,0:T(8,128)}) custom-call(bf16[2,256,512]{2,1,0:T(8,128)(2,1)} %get-tuple-element.10.tok_ref, bf16[43,3,256,128]{3,2,1,0:T(8,128)(2,1)} %get-tuple-element.12.act_ref), custom_call_target="tpu_custom_call" | custom-call | flops 2885681152 | bytes 31000000 | tf_op jit(solution)/shard_map/gate_up_grads/pallas_call | solution.py:302
  162.0 0.0 all-to-all-done
  162.1 0.1 copy.16
  162.1 0.7 squeeze.17
  162.9 0.1 copy.17
  162.9 0.7 squeeze.18
  (2 shorter events, 0.1 us)
Async XLA Ops:
  127.8 14.4 %collective-permute-start = (f32[2,2,8,8,512]{4,3,1,0,2:T(8,128)S(1)}, f32[2,2,8,8,512]{4,3,1,0,2:T(8,128)S(1)}, u32[]{:S(2)}, u32[]{:S(2)}) collective-permute-start(f32[2,2,8,8,512]{4,3,1,0,2:T(8,128)S(1)} %bitcast.28), channel_id=1, source_target_pairs={{0,8},{8,0},{1,9},{9,1},{2,10},{10,2},{3,11},{11,3},{4,12},{12,4},... | collective-permute-start | bytes 1572872 | tf_op jit(solution)/shard_map/ppermute | solution.py:331
  129.4 12.8 %copy-start = (bf16[2,256,512]{2,1,0:T(8,128)(2,1)S(1)}, bf16[2,256,512]{2,1,0:T(8,128)(2,1)}, u32[]{:S(2)}) copy-start(bf16[2,256,512]{2,1,0:T(8,128)(2,1)} %get-tuple-element.10.tok_ref) | copy-start | bytes 1572868
  143.1 19.0 %all-to-all-start = ((bf16[2,2,8,8,512]{4,3,1,0,2:T(8,128)(2,1)}), bf16[2,2,8,8,512]{4,3,1,0,2:T(8,128)(2,1)S(1)}, u32[]{:S(2)}, u32[]{:S(2)}) async-start(bf16[2,2,8,8,512]{4,3,1,0,2:T(8,128)(2,1)} %fusion), calls=%async_computation | async-start | bytes 524288 | tf_op jit(solution)/shard_map/all_to_all | solution.py:334

commit v2 on v1

--- a/solution.py
+++ b/solution.py
@@ -25,7 +25,7 @@
 
 
 def exchange_kernel(tiles, x_hbm, dy_hbm, wg_hbm, wu_hbm, wd_hbm,
-                    act_hbm, tok_hbm, out_hbm,
+                    act_hbm, tok_hbm, sum_hbm,
                     loc, tok, rows, wg, wu, wd, part, core_in, first_out, first_in, second_out, second_in, act, acc,
                     load_sem, tok_send, tok_recv, send_sem, recv_sem, store_sem):
     tp = lax.axis_index("tp")
@@ -184,16 +184,20 @@
             copies(stage - 1, i, h).wait()
             copies(stage, i, h).start()
 
+    def add_to(arr, mb, term):
+        blocks = pl.ds(mb * 8, 8)
+        acc[arr, blocks] += term.reshape(8, 2, 8, term.shape[-1])
+
     def stage_outputs(i):
         for h in range(2):
             u, mb, t = unit(i, h)
             copies(5, i, h).wait()
             cols = pl.ds(pl.multiple_of(t * LANES, LANES), LANES)
             r = pl.ds(pl.multiple_of(mb * 128, 128), 128)
-            acc[0, r, :] += dot_f32(act[t, 0, r, :], wd[cols, :])
+            add_to(0, mb, dot_f32(act[t, 0, r, :], wd[cols, :]))
             grads = jnp.concatenate([act[t, 1, r, :], act[t, 2, r, :]], axis=1)
             pair = jnp.concatenate([wg[:, cols], wu[:, cols]], axis=1)
-            acc[1, r, :] += dot_t(grads, pair)
+            add_to(1, mb, dot_t(grads, pair))
 
             pltpu.make_async_copy(act.at[t, :, r, :], act_hbm.at[t, :, r, :], store_sem.at[0]).start()
 
@@ -220,15 +224,18 @@
 
     lax.fori_loop(0, n_iter + STARTS[6], body, 0)
 
-    out_copy = pltpu.make_async_copy(acc, out_hbm, store_sem.at[2])
-    out_copy.start()
+    sums = [pltpu.make_async_copy(acc.at[arr, pl.ds(8 * mb, 8)], sum_hbm.at[:, :, arr, mb], store_sem.at[2 + 2 * arr + mb])
+            for arr in range(2) for mb in range(2)]
+    for cp in sums:
+        cp.start()
     for mb in range(2):
         for arr in range(2):
             part15 = tok.at[arr, mb, pl.ds(0, 15)]
             pltpu.make_async_copy(part15, part15, tok_send.at[arr, mb]).wait()
     pltpu.make_async_copy(rows, tok_hbm, store_sem.at[1]).wait()
     pltpu.make_async_copy(act, act_hbm, store_sem.at[0]).wait()
-    out_copy.wait()
+    for cp in sums:
+        cp.wait()
 
 
 def exchange(x_loc, dy_loc, w_gate, w_up, w_down):
@@ -240,9 +247,9 @@
         functools.partial(exchange_kernel, tiles),
         out_shape=(jax.ShapeDtypeStruct((tiles, 3, 256, LANES), bf16),
                    jax.ShapeDtypeStruct((2, 256, d_loc), bf16),
-                   jax.ShapeDtypeStruct((2, 256, d_loc), f32)),
+                   jax.ShapeDtypeStruct((8, 2, 2, 2, 8, d_loc), f32)),
         in_specs=[any_spec] * 5,
-        out_specs=(any_spec, any_spec, any_spec),
+        out_specs=(any_spec,) * 3,
         scratch_shapes=[
             pltpu.VMEM((2, 2, 8, 4096), bf16),
             pltpu.VMEM((2, 2, 16, 8, d_loc), bf16),
@@ -257,13 +264,13 @@
             pltpu.VMEM((SLOTS, 2, 3, 16, LANES), f32),
             pltpu.VMEM((2 * tiles, 3, 16, LANES), f32),
             pltpu.VMEM((tiles, 3, 256, LANES), bf16),
-            pltpu.VMEM((2, 256, d_loc), f32),
+            pltpu.VMEM((2, 16, 2, 8, d_loc), f32),
             pltpu.SemaphoreType.DMA((5,)),
             pltpu.SemaphoreType.DMA((2, 2)),
             pltpu.SemaphoreType.DMA((2, 2)),
             pltpu.SemaphoreType.DMA((6, 2, SLOTS)),
             pltpu.SemaphoreType.DMA((6, 2, SLOTS)),
-            pltpu.SemaphoreType.DMA((3,)),
+            pltpu.SemaphoreType.DMA((6,)),
         ],
         compiler_params=pltpu.CompilerParams(collective_id=0, has_side_effects=True, vmem_limit_bytes=60 * 2**20),
         cost_estimate=pl.CostEstimate(flops=9 * 10**9, bytes_accessed=28 * 10**6, transcendentals=0),
@@ -271,50 +278,90 @@
     )(x_loc, dy_loc, w_gate, w_up, w_down)
 
 
-GROUP = 4
-
-
-def gate_up_kernel(tok_ref, act_ref, dg_ref, du_ref, xt_ref):
-    @pl.when(pl.program_id(0) == 0)
-    def _():
-        xt_ref[...] = tok_ref[0].T
-
-    for k in range(GROUP):
-        dg_ref[:, k * LANES:(k + 1) * LANES] = dot_f32(xt_ref[...], act_ref[k, 1])
-        du_ref[:, k * LANES:(k + 1) * LANES] = dot_f32(xt_ref[...], act_ref[k, 2])
-
-
-def down_kernel(tok_ref, act_ref, dd_ref):
-    for k in range(GROUP):
-        dd_ref[k * LANES:(k + 1) * LANES, :] = lax.dot_general(
-            act_ref[k, 0], tok_ref[1], TRANS_A, preferred_element_type=jnp.float32)
+OUT_SLOTS = 4
+WIDTH = 2 * LANES
+
+
+def grads_kernel(tiles, tok_hbm, act_hbm, dg_hbm, du_hbm, dd_hbm, tok, xt, act, gate, up, down, load_sem, out_sem):
+    pairs = tiles // 2
+    tok_copy = pltpu.make_async_copy(tok_hbm, tok, load_sem.at[pairs + 1])
+    tok_copy.start()
+
+    def act_copy(i, n):
+        span = pl.ds(2 * i, n)
+        return pltpu.make_async_copy(act_hbm.at[span], act.at[span], load_sem.at[i])
+
+    for i in range(pairs):
+        act_copy(i, 2).start()
+    if tiles % 2:
+        act_copy(pairs, 1).start()
+    tok_copy.wait()
+    xt[...] = tok[0].T
+
+    def out_copies(i, slot, width):
+        cols = pl.ds(pl.multiple_of(i * WIDTH, WIDTH), width)
+        part = pl.ds(0, width)
+        return [pltpu.make_async_copy(gate.at[slot, :, part], dg_hbm.at[:, cols], out_sem.at[0, slot]),
+                pltpu.make_async_copy(up.at[slot, :, part], du_hbm.at[:, cols], out_sem.at[1, slot]),
+                pltpu.make_async_copy(down.at[slot, part, :], dd_hbm.at[cols, :], out_sem.at[2, slot])]
+
+    def step(i, n):
+        slot = lax.rem(i, OUT_SLOTS)
+        act_copy(i, n).wait()
+
+        def wait_old():
+            for cp in out_copies(i - OUT_SLOTS, slot, WIDTH):
+                cp.wait()
+
+        pl.when(i >= OUT_SLOTS)(wait_old)
+
+        def cols(kind):
+            return jnp.concatenate([act[2 * i + k, kind] for k in range(n)], axis=1)
+
+        part = slice(0, n * LANES)
+        gate[slot, :, part] = dot_f32(xt[...], cols(1))
+        up[slot, :, part] = dot_f32(xt[...], cols(2))
+        down[slot, part, :] = lax.dot_general(cols(0), tok[1], TRANS_A, preferred_element_type=jnp.float32)
+        for cp in out_copies(i, slot, n * LANES):
+            cp.start()
+
+    def body(i, carry):
+        step(i, 2)
+        return carry
+
+    lax.fori_loop(0, pairs, body, 0)
+    last = pairs
+    if tiles % 2:
+        step(pairs, 1)
+        last = pairs + 1
+    for i in range(last - OUT_SLOTS, last):
+        for cp in out_copies(i, i % OUT_SLOTS, WIDTH if i < pairs else LANES):
+            cp.wait()
 
 
 def weight_grads(tok, act):
     tiles = act.shape[0]
     d_loc = tok.shape[-1]
     f_loc = tiles * LANES
-    grid = (pl.cdiv(tiles, GROUP),)
-    tok_spec = pl.BlockSpec((2, 256, d_loc), lambda i: (0, 0, 0))
-    act_spec = pl.BlockSpec((GROUP, 3, 256, LANES), lambda i: (i, 0, 0, 0))
-    flops = 2 * 256 * d_loc * f_loc
-    width = GROUP * LANES
-    dg, du = pl.pallas_call(
-        gate_up_kernel, grid=grid, in_specs=[tok_spec, act_spec],
-        out_specs=[pl.BlockSpec((d_loc, width), lambda i: (0, i))] * 2,
-        out_shape=[jax.ShapeDtypeStruct((d_loc, f_loc), jnp.float32)] * 2,
-        scratch_shapes=[pltpu.VMEM((d_loc, 256), jnp.bfloat16)],
-        cost_estimate=pl.CostEstimate(flops=2 * flops, bytes_accessed=31 * 10**6, transcendentals=0),
-        name="gate_up_grads",
+    any_spec = pl.BlockSpec(memory_space=pl.ANY)
+    f32, bf16 = jnp.float32, jnp.bfloat16
+    return pl.pallas_call(
+        functools.partial(grads_kernel, tiles), in_specs=[any_spec] * 2, out_specs=[any_spec] * 3,
+        out_shape=[jax.ShapeDtypeStruct((d_loc, f_loc), f32)] * 2 + [jax.ShapeDtypeStruct((f_loc, d_loc), f32)],
+        scratch_shapes=[
+            pltpu.VMEM((2, 256, d_loc), bf16),
+            pltpu.VMEM((d_loc, 256), bf16),
+            pltpu.VMEM(act.shape, bf16),
+            pltpu.VMEM((OUT_SLOTS, d_loc, WIDTH), f32),
+            pltpu.VMEM((OUT_SLOTS, d_loc, WIDTH), f32),
+            pltpu.VMEM((OUT_SLOTS, WIDTH, d_loc), f32),
+            pltpu.SemaphoreType.DMA((tiles // 2 + 2,)),
+            pltpu.SemaphoreType.DMA((3, OUT_SLOTS)),
+        ],
+        compiler_params=pltpu.CompilerParams(vmem_limit_bytes=62 * 2**20),
+        cost_estimate=pl.CostEstimate(flops=6 * 256 * d_loc * f_loc, bytes_accessed=44 * 10**6, transcendentals=0),
+        name="weight_grads",
     )(tok, act)
-    dd = pl.pallas_call(
-        down_kernel, grid=grid, in_specs=[tok_spec, act_spec],
-        out_specs=pl.BlockSpec((width, d_loc), lambda i: (i, 0)),
-        out_shape=jax.ShapeDtypeStruct((f_loc, d_loc), jnp.float32),
-        cost_estimate=pl.CostEstimate(flops=flops, bytes_accessed=16 * 10**6, transcendentals=0),
-        name="down_grads",
-    )(tok, act)
-    return dg, du, dd
 
 
 def solution(mesh):
@@ -324,16 +371,12 @@
 
     def local_step(x_loc, w_gate, w_up, w_down, dy_loc):
         act, tok, part = exchange(x_loc, dy_loc, w_gate, w_up, w_down)
-        tp = lax.axis_index("tp")
-        part = part.reshape(2, 2, 8, 2, 8, 512)
-        keep = lax.dynamic_index_in_dim(part, tp, axis=3, keepdims=False)
-        send = lax.dynamic_index_in_dim(part, 1 - tp, axis=3, keepdims=False)
-        recv = lax.ppermute(send, "tp", [(0, 1), (1, 0)])
-        base = lax.dynamic_index_in_dim(tok.reshape(2, 2, 8, 2, 8, 512), tp, axis=3, keepdims=False)
-        out = (base.astype(jnp.float32) + (keep + recv)).astype(jnp.bfloat16)
-        out = lax.all_to_all(out, "dp", split_axis=2, concat_axis=4, tiled=True)
-        out = out.reshape(2, 2, 8, 4096)
+        part = lax.all_to_all(part.reshape(16, 2, 2, 8, -1), ("dp", "tp"), split_axis=0, concat_axis=0, tiled=True)
+        part = part.reshape(8, 2, 2, 2, 8, -1)
+        out = (part[:, 0] + part[:, 1]).transpose(1, 2, 3, 0, 4).reshape(2, 2, 8, 4096)
+        y = (x_loc.astype(jnp.float32) + out[0]).astype(jnp.bfloat16)
+        dx = (dy_loc.astype(jnp.float32) + out[1]).astype(jnp.bfloat16)
         dg, du, dd = weight_grads(tok, act)
-        return out[0], out[1], dg, du, dd
+        return y, dx, dg, du, dd
 
     return jax.shard_map(local_step, mesh=mesh, in_specs=in_specs, out_specs=out_specs, check_vma=False)

time: 165 us -> 146 us (0.88)
  Pallas kernels: 154 us -> 139 us
  local copies, waits for them, and re-layouts: 2.95 us -> 0.15 us
  starting transfers between devices: 4.96 us -> 2.41 us
  waiting for transfers between devices: 0.01 us -> 2.22 us
    pallas_call x2 -> x1, Pallas kernels: 28.4 us -> 13.6 us  [weight_grads(): pl.pallas_call(functools.partial(grads_kernel, tiles), in_specs=[any_spec...]
    all_to_all x1, waiting for transfers between devices: 0.01 us -> 2.22 us  [local_step(): lax.all_to_all(part.reshape(16, 2, 2, 8, -1), ('dp', 'tp'), split_axis=0,...]
  transfers between devices with their start and end apart: 2 -> 1, of which waited for: 0 -> 1; matrix products, arithmetic and copies ran while one was open for 0% -> 0% of each run, Pallas kernels for 17% -> 9%
where the time goes in v2:
time: 146 us
  Pallas kernels  139 us (95%)
  starting transfers between devices  2.41 us (2%)
  waiting for transfers between devices  2.22 us (2%)
    pallas_call x1, Pallas kernels, exchange(): pl.pallas_call(functools.partial(exchange_kernel, tiles), out_shape=(jax....  126 us
    pallas_call x1, Pallas kernels, weight_grads(): pl.pallas_call(functools.partial(grads_kernel, tiles), in_specs=[any_spec...  13.6 us
  transfers between devices with their start and end apart: 1, of which 1 were waited for; matrix products, arithmetic and copies ran while one was open for 0% of the time, Pallas kernels for 9%

profile of v2, /device:TPU:0, one launch (start us, length us, event | category | flops | bytes accessed | tf_op | source)
XLA Modules:
  0.0 145.8 jit_solution(14988229363648370256)
XLA Ops:
  0.6 125.9 %exchange.1 = (bf16[43,3,256,128]{3,2,1,0:T(8,128)(2,1)}, bf16[2,256,512]{2,1,0:T(8,128)(2,1)}, f32[8,2,2,2,8,512]{5,4,3,2,1,0:T(8,128)}) custom-call(bf16[2,8,4096]{2,1,0:T(8,128)(2,1)} %x_hbm.1, bf16[2,8,4096]{2,1,0:T(8,128)(2,1)} %dy_hbm.1, bf16[512,5504]{1,0:T(8,128)(2,1)} %wg_hbm.1, bf16[512,5504]{1,0:T(8,128)(2,1)} %wu_hbm.1, bf16[5504,512]{1,0:T(8,128)(2,1)} %wd_hbm.1), custom_call_target="tpu_custom_call" | custom-call | flops 8999999488 | bytes 28000000 | tf_op jit(solution)/shard_map/exchange/pallas_call | solution.py:246
  126.5 2.4 %all-to-all-start = ((f32[16,2,2,8,512]{4,3,2,1,0:T(8,128)}), f32[16,2,2,8,512]{4,3,2,1,0:T(8,128)S(1)}, u32[]{:S(2)}, u32[]{:S(2)}) async-start(f32[16,2,2,8,512]{4,3,2,1,0:T(8,128)} %bitcast.9), calls=%async_computation | async-start | bytes 2097152 | tf_op jit(solution)/shard_map/all_to_all | solution.py:374
  128.9 0.0 copy-start
  128.9 0.0 copy-start.1
  128.9 13.6 %weight_grads.1 = (f32[512,5504]{1,0:T(8,128)}, f32[512,5504]{1,0:T(8,128)}, f32[5504,512]{1,0:T(8,128)}) custom-call(bf16[2,256,512]{2,1,0:T(8,128)(2,1)} %get-tuple-element.12.tok_hbm, bf16[43,3,256,128]{3,2,1,0:T(8,128)(2,1)} %get-tuple-element.13.act_hbm), custom_call_target="tpu_custom_call" | custom-call | flops 4328521728 | bytes 44000000 | tf_op jit(solution)/shard_map/weight_grads/pallas_call | solution.py:348
  142.5 2.2 %all-to-all-done = f32[16,2,2,8,512]{4,3,2,1,0:T(8,128)S(1)} async-done(((f32[16,2,2,8,512]{4,3,2,1,0:T(8,128)}), f32[16,2,2,8,512]{4,3,2,1,0:T(8,128)S(1)}, u32[]{:S(2)}, u32[]{:S(2)}) %all-to-all-start) | async-done | bytes 1048608 | tf_op jit(solution)/shard_map/all_to_all | solution.py:374
  144.8 0.1 fusion.1
  144.9 0.1 fusion
  145.0 0.0 copy-done
  145.0 0.0 copy-done.1
  145.0 0.8 add_convert_fusion
  (1 shorter events, 0.0 us)
Async XLA Ops:
  126.5 18.3 %all-to-all-start = ((f32[16,2,2,8,512]{4,3,2,1,0:T(8,128)}), f32[16,2,2,8,512]{4,3,2,1,0:T(8,128)S(1)}, u32[]{:S(2)}, u32[]{:S(2)}) async-start(f32[16,2,2,8,512]{4,3,2,1,0:T(8,128)} %bitcast.9), calls=%async_computation | async-start | bytes 2097152 | tf_op jit(solution)/shard_map/all_to_all | solution.py:374
  128.9 16.1 %copy-start = (bf16[2,8,4096]{2,1,0:T(8,128)(2,1)S(1)}, bf16[2,8,4096]{2,1,0:T(8,128)(2,1)}, u32[]{:S(2)}) copy-start(bf16[2,8,4096]{2,1,0:T(8,128)(2,1)} %x_hbm.1) | copy-start | bytes 393220
  128.9 16.1 %copy-start.1 = (bf16[2,8,4096]{2,1,0:T(8,128)(2,1)S(1)}, bf16[2,8,4096]{2,1,0:T(8,128)(2,1)}, u32[]{:S(2)}) copy-start(bf16[2,8,4096]{2,1,0:T(8,128)(2,1)} %dy_hbm.1) | copy-start | bytes 393220

commit v3 on v2

--- a/solution.py
+++ b/solution.py
@@ -25,9 +25,9 @@
 
 
 def exchange_kernel(tiles, x_hbm, dy_hbm, wg_hbm, wu_hbm, wd_hbm,
-                    act_hbm, tok_hbm, sum_hbm,
-                    loc, tok, rows, wg, wu, wd, part, core_in, first_out, first_in, second_out, second_in, act, acc,
-                    load_sem, tok_send, tok_recv, send_sem, recv_sem, store_sem):
+                    act_hbm, tok_hbm, sum_hbm, first_hbm,
+                    loc, tok, rows, wg, wu, wd, part, core_in, first_out, first_in, second_out, second_in, act, acc, zin, fin, yin,
+                    load_sem, tok_send, tok_recv, send_sem, recv_sem, store_sem, z_sem, fin_sem):
     tp = lax.axis_index("tp")
     dp = lax.axis_index("dp")
     core = lax.rem(dp, 2)
@@ -53,7 +53,7 @@
     for cp in token_loads + weight_loads:
         cp.start()
 
-    others = [((k >> 0) & 1, (k >> 1) & 1, (k >> 2) & 1, (k >> 3) & 1) for k in range(1, 16)]
+    others = [((k >> 0) & 1, (k >> 1) & 1, (k >> 2) & 1, (k >> 3) & 1) for k in range(15, 0, -1)]
     barrier = pltpu.get_barrier_semaphore()
     for flags in others:
         pl.semaphore_signal(barrier, 1, device_id=device(*flags), device_id_type=MESH)
@@ -201,7 +201,34 @@
 
             pltpu.make_async_copy(act.at[t, :, r, :], act_hbm.at[t, :, r, :], store_sem.at[0]).start()
 
+    z_copy = pltpu.make_async_remote_copy(
+        src_ref=acc.at[:, pl.ds(0, 8), 1 - tp], dst_ref=zin, send_sem=z_sem.at[0], recv_sem=z_sem.at[1],
+        device_id=device(0, 0, 0, 1), device_id_type=MESH)
+    plane = [flags for flags in others if not flags[3]]
+    my_cols = pl.ds(pl.multiple_of(dp * 512, 512), 512)
+
+    def finish_first():
+        z_copy.wait()
+        for arr in range(2):
+            for blk in range(8):
+                total = acc[arr, blk, tp] + zin[arr, blk]
+                fin[blk, arr] = (tok[arr, 0, 2 * blk + tp].astype(jnp.float32) + total).astype(jnp.bfloat16)
+
+    def send_first():
+        for flags in plane:
+            dest = device(*flags)
+            pltpu.make_async_remote_copy(
+                src_ref=fin.at[dest[1]], dst_ref=yin.at[:, :, my_cols], send_sem=fin_sem.at[0], recv_sem=fin_sem.at[1],
+                device_id=dest, device_id_type=MESH).start()
+        yin[:, :, my_cols] = fin[dp]
+
+    z_start = (tiles - 1) // 2 + STARTS[6] + 1
+
     def body(j, carry):
+        pl.when(j == z_start)(z_copy.start)
+        pl.when(j == z_start + 8)(finish_first)
+        pl.when(j == n_iter + 4)(send_first)
+
         def run(stage, fn):
             i = j - STARTS[stage]
             pl.when(jnp.logical_and(i >= 0, i < n_iter))(functools.partial(fn, i))
@@ -224,10 +251,14 @@
 
     lax.fori_loop(0, n_iter + STARTS[6], body, 0)
 
-    sums = [pltpu.make_async_copy(acc.at[arr, pl.ds(8 * mb, 8)], sum_hbm.at[:, :, arr, mb], store_sem.at[2 + 2 * arr + mb])
-            for arr in range(2) for mb in range(2)]
+    sums = [pltpu.make_async_copy(acc.at[arr, pl.ds(8, 8)], sum_hbm.at[:, :, arr], store_sem.at[2 + arr]) for arr in range(2)]
     for cp in sums:
         cp.start()
+    blocks = fin.at[pl.ds(0, 7)]
+    for k in range(2):
+        pltpu.make_async_copy(blocks, blocks, fin_sem.at[k]).wait()
+    first_copy = pltpu.make_async_copy(yin, first_hbm, store_sem.at[4])
+    first_copy.start()
     for mb in range(2):
         for arr in range(2):
             part15 = tok.at[arr, mb, pl.ds(0, 15)]
@@ -236,6 +267,7 @@
     pltpu.make_async_copy(act, act_hbm, store_sem.at[0]).wait()
     for cp in sums:
         cp.wait()
+    first_copy.wait()
 
 
 def exchange(x_loc, dy_loc, w_gate, w_up, w_down):
@@ -247,9 +279,10 @@
         functools.partial(exchange_kernel, tiles),
         out_shape=(jax.ShapeDtypeStruct((tiles, 3, 256, LANES), bf16),
                    jax.ShapeDtypeStruct((2, 256, d_loc), bf16),
-                   jax.ShapeDtypeStruct((8, 2, 2, 2, 8, d_loc), f32)),
+                   jax.ShapeDtypeStruct((8, 2, 2, 8, d_loc), f32),
+                   jax.ShapeDtypeStruct((2, 8, 4096), bf16)),
         in_specs=[any_spec] * 5,
-        out_specs=(any_spec,) * 3,
+        out_specs=(any_spec,) * 4,
         scratch_shapes=[
             pltpu.VMEM((2, 2, 8, 4096), bf16),
             pltpu.VMEM((2, 2, 16, 8, d_loc), bf16),
@@ -265,12 +298,17 @@
             pltpu.VMEM((2 * tiles, 3, 16, LANES), f32),
             pltpu.VMEM((tiles, 3, 256, LANES), bf16),
             pltpu.VMEM((2, 16, 2, 8, d_loc), f32),
+            pltpu.VMEM((2, 8, 8, d_loc), f32),
+            pltpu.VMEM((8, 2, 8, d_loc), bf16),
+            pltpu.VMEM((2, 8, 4096), bf16),
             pltpu.SemaphoreType.DMA((5,)),
             pltpu.SemaphoreType.DMA((2, 2)),
             pltpu.SemaphoreType.DMA((2, 2)),
             pltpu.SemaphoreType.DMA((6, 2, SLOTS)),
             pltpu.SemaphoreType.DMA((6, 2, SLOTS)),
-            pltpu.SemaphoreType.DMA((6,)),
+            pltpu.SemaphoreType.DMA((5,)),
+            pltpu.SemaphoreType.DMA((2,)),
+            pltpu.SemaphoreType.DMA((2,)),
         ],
         compiler_params=pltpu.CompilerParams(collective_id=0, has_side_effects=True, vmem_limit_bytes=60 * 2**20),
         cost_estimate=pl.CostEstimate(flops=9 * 10**9, bytes_accessed=28 * 10**6, transcendentals=0),
@@ -370,12 +408,12 @@
     out_specs = (row_spec, row_spec, P("dp", "tp"), P("dp", "tp"), P("tp", "dp"))
 
     def local_step(x_loc, w_gate, w_up, w_down, dy_loc):
-        act, tok, part = exchange(x_loc, dy_loc, w_gate, w_up, w_down)
-        part = lax.all_to_all(part.reshape(16, 2, 2, 8, -1), ("dp", "tp"), split_axis=0, concat_axis=0, tiled=True)
-        part = part.reshape(8, 2, 2, 2, 8, -1)
-        out = (part[:, 0] + part[:, 1]).transpose(1, 2, 3, 0, 4).reshape(2, 2, 8, 4096)
-        y = (x_loc.astype(jnp.float32) + out[0]).astype(jnp.bfloat16)
-        dx = (dy_loc.astype(jnp.float32) + out[1]).astype(jnp.bfloat16)
+        act, tok, part, first = exchange(x_loc, dy_loc, w_gate, w_up, w_down)
+        part = lax.all_to_all(part.reshape(16, 2, 8, -1), ("dp", "tp"), split_axis=0, concat_axis=0, tiled=True)
+        part = part.reshape(8, 2, 2, 8, -1)
+        out = (part[:, 0] + part[:, 1]).transpose(1, 2, 0, 3).reshape(2, 8, 4096)
+        y = jnp.stack([first[0], (x_loc[1].astype(jnp.float32) + out[0]).astype(jnp.bfloat16)])
+        dx = jnp.stack([first[1], (dy_loc[1].astype(jnp.float32) + out[1]).astype(jnp.bfloat16)])
         dg, du, dd = weight_grads(tok, act)
         return y, dx, dg, du, dd
 

time: 146 us -> 144 us (0.986)
  waiting for transfers between devices: 2.22 us -> 0.01 us
    all_to_all x1, waiting for transfers between devices: 2.22 us -> 0.01 us  [local_step(): lax.all_to_all(part.reshape(16, 2, 8, -1), ('dp', 'tp'), split_axis=0, co...]
  transfers between devices with their start and end apart: 1 -> 1, of which waited for: 1 -> 0; matrix products, arithmetic and copies ran while one was open for 0% -> 1% of each run, Pallas kernels for 9% -> 9%
where the time goes in v3:
time: 144 us
  Pallas kernels  139 us (97%)
  starting transfers between devices  2.33 us (2%)
    pallas_call x1, Pallas kernels, exchange(): pl.pallas_call(functools.partial(exchange_kernel, tiles), out_shape=(jax....  126 us
    pallas_call x1, Pallas kernels, weight_grads(): pl.pallas_call(functools.partial(grads_kernel, tiles), in_specs=[any_spec...  13.6 us
  transfers between devices with their start and end apart: 1, of which 0 were waited for; matrix products, arithmetic and copies ran while one was open for 1% of the time, Pallas kernels for 9%

profile of v3, /device:TPU:0, one launch (start us, length us, event | category | flops | bytes accessed | tf_op | source)
XLA Modules:
  0.0 144.1 jit_solution(8924787877871586423)
XLA Ops:
  0.6 125.8 %exchange.1 = (bf16[43,3,256,128]{3,2,1,0:T(8,128)(2,1)}, bf16[2,256,512]{2,1,0:T(8,128)(2,1)}, f32[8,2,2,8,512]{4,3,2,1,0:T(8,128)}, bf16[2,8,4096]{2,1,0:T(8,128)(2,1)}) custom-call(bf16[2,8,4096]{2,1,0:T(8,128)(2,1)} %x_hbm.1, bf16[2,8,4096]{2,1,0:T(8,128)(2,1)} %dy_hbm.1, bf16[512,5504]{1,0:T(8,128)(2,1)} %wg_hbm.1, bf16[512,5504]{1,0:T(8,128)(2,1)} %wu_hbm.1, ...), custom_call_target="tpu_custom_call" | custom-call | flops 8999999488 | bytes 28000000 | tf_op jit(solution)/shard_map/exchange/pallas_call | solution.py:278
  126.4 2.3 %all-to-all-start = ((f32[16,2,8,512]{3,2,1,0:T(8,128)}), f32[16,2,8,512]{3,2,1,0:T(8,128)S(1)}, u32[]{:S(2)}, u32[]{:S(2)}) async-start(f32[16,2,8,512]{3,2,1,0:T(8,128)} %bitcast.9), calls=%async_computation | async-start | bytes 1048576 | tf_op jit(solution)/shard_map/all_to_all | solution.py:412
  128.7 0.9 fusion.2
  129.6 0.0 copy-start
  129.6 0.0 copy-start.1
  129.7 13.6 %weight_grads.1 = (f32[512,5504]{1,0:T(8,128)}, f32[512,5504]{1,0:T(8,128)}, f32[5504,512]{1,0:T(8,128)}) custom-call(bf16[2,256,512]{2,1,0:T(8,128)(2,1)} %get-tuple-element.14.tok_hbm, bf16[43,3,256,128]{3,2,1,0:T(8,128)(2,1)} %get-tuple-element.15.act_hbm), custom_call_target="tpu_custom_call" | custom-call | flops 4328521728 | bytes 44000000 | tf_op jit(solution)/shard_map/weight_grads/pallas_call | solution.py:386
  143.3 0.0 all-to-all-done
  143.3 0.0 copy-done
  143.4 0.0 copy-done.1
  143.4 0.7 pad_maximum_fusion
  (4 shorter events, 0.1 us)
Async XLA Ops:
  126.4 16.8 %all-to-all-start = ((f32[16,2,8,512]{3,2,1,0:T(8,128)}), f32[16,2,8,512]{3,2,1,0:T(8,128)S(1)}, u32[]{:S(2)}, u32[]{:S(2)}) async-start(f32[16,2,8,512]{3,2,1,0:T(8,128)} %bitcast.9), calls=%async_computation | async-start | bytes 1048576 | tf_op jit(solution)/shard_map/all_to_all | solution.py:412
  129.6 13.7 %copy-start = (bf16[2,8,4096]{2,1,0:T(8,128)(2,1)S(1)}, bf16[2,8,4096]{2,1,0:T(8,128)(2,1)}, u32[]{:S(2)}) copy-start(bf16[2,8,4096]{2,1,0:T(8,128)(2,1)} %dy_hbm.1) | copy-start | bytes 393220
  129.6 13.7 %copy-start.1 = (bf16[2,8,4096]{2,1,0:T(8,128)(2,1)S(1)}, bf16[2,8,4096]{2,1,0:T(8,128)(2,1)}, u32[]{:S(2)}) copy-start(bf16[2,8,4096]{2,1,0:T(8,128)(2,1)} %x_hbm.1) | copy-start | bytes 393220

commit v4 on v3

--- a/solution.py
+++ b/solution.py
@@ -10,6 +10,8 @@
 MESH = pl.DeviceIdType.MESH
 LANES = 128
 SLOTS = 8
+LATE_SLOTS = 16
+DEFER = 7
 LAGS = (1, 2, 2, 2, 2, 1)
 STARTS = tuple(sum(LAGS[:k]) for k in range(len(LAGS) + 1))
 TRANS_B = (((1,), (1,)), ((), ()))
@@ -25,9 +27,9 @@
 
 
 def exchange_kernel(tiles, x_hbm, dy_hbm, wg_hbm, wu_hbm, wd_hbm,
-                    act_hbm, tok_hbm, sum_hbm, first_hbm,
+                    act_hbm, tok_hbm, sum_hbm, y_hbm, dx_hbm,
                     loc, tok, rows, wg, wu, wd, part, core_in, first_out, first_in, second_out, second_in, act, acc, zin, fin, yin,
-                    load_sem, tok_send, tok_recv, send_sem, recv_sem, store_sem, z_sem, fin_sem):
+                    load_sem, tok_send, tok_recv, send_sem, recv_sem, late_sem, gather_sem, store_sem, z_sem, fin_sem):
     tp = lax.axis_index("tp")
     dp = lax.axis_index("dp")
     core = lax.rem(dp, 2)
@@ -125,8 +127,25 @@
             src = dst = act.at[t, :, pl.ds(off(base), 64), :]
             dev = core_peer
         return pltpu.make_async_remote_copy(
-            src_ref=src, dst_ref=dst, send_sem=send_sem.at[stage, h, slot], recv_sem=recv_sem.at[stage, h, slot],
-            device_id=dev, device_id_type=MESH)
+            src_ref=src, dst_ref=dst, send_sem=send_sem.at[stage, slot] if stage < 3 else gather_sem.at[0],
+            recv_sem=arrival(stage, i), device_id=dev, device_id_type=MESH)
+
+    def arrival(stage, i):
+        if stage < 3:
+            return recv_sem.at[stage, lax.rem(i, SLOTS)]
+        return late_sem.at[stage - 3, lax.rem(i, LATE_SLOTS)]
+
+    def start_pair(stage, i):
+        for h in range(2):
+            copies(stage, i, h).start()
+
+    def wait_pair(stage, i):
+        if stage < 3:
+            into = (core_in, first_in, second_in)[stage].at[pl.ds(2 * i, 2)]
+            pltpu.make_async_copy(into, into, send_sem.at[stage, lax.rem(i, SLOTS)]).wait()
+        else:
+            into = act.at[0, :, pl.ds(0, 32 << (stage - 3)), :]
+        pltpu.make_async_copy(into, into, arrival(stage, i)).wait()
 
     def stage_partials(i):
         for h in range(2):
@@ -139,22 +158,22 @@
             part[slot, h, 0] = ab[:, :LANES]
             part[slot, h, 1] = ab[:, LANES:]
             part[slot, h, 2] = dot_t(rows[1, r, :], wd[cols, :])
-            copies(0, i, h).start()
+        start_pair(0, i)
 
     def stage_first(i):
         slot = lax.rem(i, SLOTS)
+        wait_pair(0, i)
         for h in range(2):
             u, _, _ = unit(i, h)
-            copies(0, i, h).wait()
             o = (1 - pos1[h]) * 32
             first_out[slot, h] = (part[slot, h, :, pl.ds(off(core * 64 + o), 32), :] + core_in[u, :, pl.ds(off(o), 32), :])
             copies(1, i, h).start()
 
     def stage_second(i):
         slot = lax.rem(i, SLOTS)
+        wait_pair(1, i)
         for h in range(2):
             u, _, _ = unit(i, h)
-            copies(1, i, h).wait()
             o2 = (1 - pos2[h]) * 16
             o = pos1[h] * 32 + o2
             second_out[slot, h] = (part[slot, h, :, pl.ds(off(core * 64 + o), 16), :] + core_in[u, :, pl.ds(off(o), 16), :]
@@ -163,9 +182,9 @@
 
     def stage_act(i):
         slot = lax.rem(i, SLOTS)
+        wait_pair(2, i)
         for h in range(2):
             u, mb, t = unit(i, h)
-            copies(2, i, h).wait()
             o2 = pos2[h] * 16
             o = pos1[h] * 32 + o2
             tot = (part[slot, h, :, pl.ds(off(core * 64 + o), 16), :] + core_in[u, :, pl.ds(off(o), 16), :]
@@ -180,18 +199,17 @@
             copies(3, i, h).start()
 
     def stage_forward(stage, i):
-        for h in range(2):
-            copies(stage - 1, i, h).wait()
-            copies(stage, i, h).start()
+        wait_pair(stage - 1, i)
+        start_pair(stage, i)
 
     def add_to(arr, mb, term):
         blocks = pl.ds(mb * 8, 8)
         acc[arr, blocks] += term.reshape(8, 2, 8, term.shape[-1])
 
     def stage_outputs(i):
+        wait_pair(5, i)
         for h in range(2):
             u, mb, t = unit(i, h)
-            copies(5, i, h).wait()
             cols = pl.ds(pl.multiple_of(t * LANES, LANES), LANES)
             r = pl.ds(pl.multiple_of(mb * 128, 128), 128)
             add_to(0, mb, dot_f32(act[t, 0, r, :], wd[cols, :]))
@@ -222,22 +240,34 @@
                 device_id=dest, device_id_type=MESH).start()
         yin[:, :, my_cols] = fin[dp]
 
-    z_start = (tiles - 1) // 2 + STARTS[6] + 1
+    z_start = (tiles - 1) // 2 + STARTS[6] + DEFER + 1
+
+    def forwarded(j):
+        ready = jnp.maximum(j - STARTS[4] + 1, 0)
+        late = jnp.maximum(j - STARTS[4] + 1 - DEFER, 0) + jnp.maximum(j - n_iter + 1, 0)
+        return jnp.minimum(n_iter, jnp.minimum(ready, late))
+
+    def run_late(j, fn):
+        def step(i, carry):
+            fn(i)
+            return carry
+
+        lax.fori_loop(forwarded(j - 1), forwarded(j), step, 0)
 
     def body(j, carry):
         pl.when(j == z_start)(z_copy.start)
-        pl.when(j == z_start + 8)(finish_first)
+        pl.when(j == z_start + 5)(finish_first)
         pl.when(j == n_iter + 4)(send_first)
 
         def run(stage, fn):
             i = j - STARTS[stage]
             pl.when(jnp.logical_and(i >= 0, i < n_iter))(functools.partial(fn, i))
 
-        run(5, functools.partial(stage_forward, 5))
-        run(4, functools.partial(stage_forward, 4))
         run(3, stage_act)
         run(2, stage_second)
         run(1, stage_first)
+        run_late(j, functools.partial(stage_forward, 4))
+        run_late(j - LAGS[4], functools.partial(stage_forward, 5))
 
         @pl.when(j == tiles // 2 - 2)
         def _():
@@ -246,7 +276,7 @@
             pltpu.make_async_copy(rows, tok_hbm, store_sem.at[1]).start()
 
         run(0, stage_partials)
-        run(6, stage_outputs)
+        run_late(j - LAGS[4] - LAGS[5], stage_outputs)
         return carry
 
     lax.fori_loop(0, n_iter + STARTS[6], body, 0)
@@ -257,17 +287,19 @@
     blocks = fin.at[pl.ds(0, 7)]
     for k in range(2):
         pltpu.make_async_copy(blocks, blocks, fin_sem.at[k]).wait()
-    first_copy = pltpu.make_async_copy(yin, first_hbm, store_sem.at[4])
-    first_copy.start()
+    firsts = [pltpu.make_async_copy(yin.at[k], ref, store_sem.at[4 + k]) for k, ref in enumerate((y_hbm, dx_hbm))]
+    for cp in firsts:
+        cp.start()
     for mb in range(2):
         for arr in range(2):
             part15 = tok.at[arr, mb, pl.ds(0, 15)]
             pltpu.make_async_copy(part15, part15, tok_send.at[arr, mb]).wait()
     pltpu.make_async_copy(rows, tok_hbm, store_sem.at[1]).wait()
     pltpu.make_async_copy(act, act_hbm, store_sem.at[0]).wait()
-    for cp in sums:
+    sent = act.at[:, :, pl.ds(0, 224), :]
+    pltpu.make_async_copy(sent, sent, gather_sem.at[0]).wait()
+    for cp in sums + firsts:
         cp.wait()
-    first_copy.wait()
 
 
 def exchange(x_loc, dy_loc, w_gate, w_up, w_down):
@@ -280,9 +312,9 @@
         out_shape=(jax.ShapeDtypeStruct((tiles, 3, 256, LANES), bf16),
                    jax.ShapeDtypeStruct((2, 256, d_loc), bf16),
                    jax.ShapeDtypeStruct((8, 2, 2, 8, d_loc), f32),
-                   jax.ShapeDtypeStruct((2, 8, 4096), bf16)),
+                   *[jax.ShapeDtypeStruct((8, 4096), bf16)] * 2),
         in_specs=[any_spec] * 5,
-        out_specs=(any_spec,) * 4,
+        out_specs=(any_spec,) * 5,
         scratch_shapes=[
             pltpu.VMEM((2, 2, 8, 4096), bf16),
             pltpu.VMEM((2, 2, 16, 8, d_loc), bf16),
@@ -304,9 +336,11 @@
             pltpu.SemaphoreType.DMA((5,)),
             pltpu.SemaphoreType.DMA((2, 2)),
             pltpu.SemaphoreType.DMA((2, 2)),
-            pltpu.SemaphoreType.DMA((6, 2, SLOTS)),
-            pltpu.SemaphoreType.DMA((6, 2, SLOTS)),
-            pltpu.SemaphoreType.DMA((5,)),
+            pltpu.SemaphoreType.DMA((3, SLOTS)),
+            pltpu.SemaphoreType.DMA((3, SLOTS)),
+            pltpu.SemaphoreType.DMA((3, LATE_SLOTS)),
+            pltpu.SemaphoreType.DMA((1,)),
+            pltpu.SemaphoreType.DMA((6,)),
             pltpu.SemaphoreType.DMA((2,)),
             pltpu.SemaphoreType.DMA((2,)),
         ],
@@ -408,12 +442,12 @@
     out_specs = (row_spec, row_spec, P("dp", "tp"), P("dp", "tp"), P("tp", "dp"))
 
     def local_step(x_loc, w_gate, w_up, w_down, dy_loc):
-        act, tok, part, first = exchange(x_loc, dy_loc, w_gate, w_up, w_down)
+        act, tok, part, y_first, dx_first = exchange(x_loc, dy_loc, w_gate, w_up, w_down)
         part = lax.all_to_all(part.reshape(16, 2, 8, -1), ("dp", "tp"), split_axis=0, concat_axis=0, tiled=True)
         part = part.reshape(8, 2, 2, 8, -1)
         out = (part[:, 0] + part[:, 1]).transpose(1, 2, 0, 3).reshape(2, 8, 4096)
-        y = jnp.stack([first[0], (x_loc[1].astype(jnp.float32) + out[0]).astype(jnp.bfloat16)])
-        dx = jnp.stack([first[1], (dy_loc[1].astype(jnp.float32) + out[1]).astype(jnp.bfloat16)])
+        y = jnp.stack([y_first, (x_loc[1].astype(jnp.float32) + out[0]).astype(jnp.bfloat16)])
+        dx = jnp.stack([dx_first, (dy_loc[1].astype(jnp.float32) + out[1]).astype(jnp.bfloat16)])
         dg, du, dd = weight_grads(tok, act)
         return y, dx, dg, du, dd
 

time: 144 us -> 141 us (0.979)
  Pallas kernels: 139 us -> 137 us
    pallas_call x1, Pallas kernels: 126 us -> 123 us  [exchange(): pl.pallas_call(functools.partial(exchange_kernel, tiles), out_shape=(jax....]
  transfers between devices with their start and end apart: 1 -> 1, of which waited for: 0 -> 0; matrix products, arithmetic and copies ran while one was open for 1% -> 0% of each run, Pallas kernels for 9% -> 10%
where the time goes in v4:
time: 141 us
  Pallas kernels  137 us (97%)
  starting transfers between devices  2.33 us (2%)
    pallas_call x1, Pallas kernels, exchange(): pl.pallas_call(functools.partial(exchange_kernel, tiles), out_shape=(jax....  123 us
    pallas_call x1, Pallas kernels, weight_grads(): pl.pallas_call(functools.partial(grads_kernel, tiles), in_specs=[any_spec...  13.6 us
  transfers between devices with their start and end apart: 1, of which 0 were waited for; matrix products, arithmetic and copies ran while one was open for 0% of the time, Pallas kernels for 10%

profile of v4, /device:TPU:0, one launch (start us, length us, event | category | flops | bytes accessed | tf_op | source)
XLA Modules:
  0.0 140.9 jit_solution(16103181092216773446)
XLA Ops:
  0.6 123.4 %exchange.1 = (bf16[43,3,256,128]{3,2,1,0:T(8,128)(2,1)}, bf16[2,256,512]{2,1,0:T(8,128)(2,1)}, f32[8,2,2,8,512]{4,3,2,1,0:T(8,128)}, bf16[8,4096]{1,0:T(8,128)(2,1)}, bf16[8,4096]{1,0:T(8,128)(2,1)}) custom-call(bf16[2,8,4096]{2,1,0:T(8,128)(2,1)} %x_hbm.1, bf16[2,8,4096]{2,1,0:T(8,128)(2,1)} %dy_hbm.1, bf16[512,5504]{1,0:T(8,128)(2,1)} %wg_hbm.1, ...), custom_call_target="tpu_custom_call" | custom-call | flops 8999999488 | bytes 28000000 | tf_op jit(solution)/shard_map/exchange/pallas_call | solution.py:310
  124.0 2.3 %all-to-all-start = ((f32[16,2,8,512]{3,2,1,0:T(8,128)}), f32[16,2,8,512]{3,2,1,0:T(8,128)S(1)}, u32[]{:S(2)}, u32[]{:S(2)}) async-start(f32[16,2,8,512]{3,2,1,0:T(8,128)} %bitcast.11), calls=%async_computation | async-start | bytes 1048576 | tf_op jit(solution)/shard_map/all_to_all | solution.py:446
  126.4 0.0 copy-start.2
  126.4 0.0 copy-start.3
  126.4 0.0 copy-start
  126.4 0.0 copy-start.1
  126.4 13.6 %weight_grads.1 = (f32[512,5504]{1,0:T(8,128)}, f32[512,5504]{1,0:T(8,128)}, f32[5504,512]{1,0:T(8,128)}) custom-call(bf16[2,256,512]{2,1,0:T(8,128)(2,1)} %get-tuple-element.16.tok_hbm, bf16[43,3,256,128]{3,2,1,0:T(8,128)(2,1)} %get-tuple-element.17.act_hbm), custom_call_target="tpu_custom_call" | custom-call | flops 4328521728 | bytes 44000000 | tf_op jit(solution)/shard_map/weight_grads/pallas_call | solution.py:420
  140.1 0.0 all-to-all-done
  140.1 0.0 copy-done.2
  140.2 0.0 copy-done.3
  140.2 0.0 copy-done
  140.2 0.0 copy-done.1
  140.2 0.7 pad_maximum_fusion
  (4 shorter events, 0.1 us)
Async XLA Ops:
  124.0 16.0 %all-to-all-start = ((f32[16,2,8,512]{3,2,1,0:T(8,128)}), f32[16,2,8,512]{3,2,1,0:T(8,128)S(1)}, u32[]{:S(2)}, u32[]{:S(2)}) async-start(f32[16,2,8,512]{3,2,1,0:T(8,128)} %bitcast.11), calls=%async_computation | async-start | bytes 1048576 | tf_op jit(solution)/shard_map/all_to_all | solution.py:446
  126.4 13.8 %copy-start.2 = (bf16[2,8,4096]{2,1,0:T(8,128)(2,1)S(1)}, bf16[2,8,4096]{2,1,0:T(8,128)(2,1)}, u32[]{:S(2)}) copy-start(bf16[2,8,4096]{2,1,0:T(8,128)(2,1)} %dy_hbm.1) | copy-start | bytes 393220
  126.4 13.8 %copy-start.3 = (bf16[2,8,4096]{2,1,0:T(8,128)(2,1)S(1)}, bf16[2,8,4096]{2,1,0:T(8,128)(2,1)}, u32[]{:S(2)}) copy-start(bf16[2,8,4096]{2,1,0:T(8,128)(2,1)} %x_hbm.1) | copy-start | bytes 393220
  126.4 13.8 %copy-start = (bf16[8,4096]{1,0:T(8,128)(2,1)S(1)}, bf16[8,4096]{1,0:T(8,128)(2,1)}, u32[]{:S(2)}) copy-start(bf16[8,4096]{1,0:T(8,128)(2,1)} %get-tuple-element.13) | copy-start | bytes 196612
  126.4 13.8 %copy-start.1 = (bf16[8,4096]{1,0:T(8,128)(2,1)S(1)}, bf16[8,4096]{1,0:T(8,128)(2,1)}, u32[]{:S(2)}) copy-start(bf16[8,4096]{1,0:T(8,128)(2,1)} %get-tuple-element.15) | copy-start | bytes 196612

commit v5 on v4

--- a/solution.py
+++ b/solution.py
@@ -11,8 +11,8 @@
 LANES = 128
 SLOTS = 8
 LATE_SLOTS = 16
-DEFER = 7
-LAGS = (1, 2, 2, 2, 2, 1)
+DEFER = 8
+LAGS = (3, 3, 2, 2, 2, 1)
 STARTS = tuple(sum(LAGS[:k]) for k in range(len(LAGS) + 1))
 TRANS_B = (((1,), (1,)), ((), ()))
 TRANS_A = (((0,), (0,)), ((), ()))
@@ -27,9 +27,9 @@
 
 
 def exchange_kernel(tiles, x_hbm, dy_hbm, wg_hbm, wu_hbm, wd_hbm,
-                    act_hbm, tok_hbm, sum_hbm, y_hbm, dx_hbm,
-                    loc, tok, rows, wg, wu, wd, part, core_in, first_out, first_in, second_out, second_in, act, acc, zin, fin, yin,
-                    load_sem, tok_send, tok_recv, send_sem, recv_sem, late_sem, gather_sem, store_sem, z_sem, fin_sem):
+                    act_hbm, xt_hbm, dy_rows_hbm, sum_hbm, y_hbm, dx_hbm,
+                    loc, tok, rows, wg, wu, wd, part, core_in, first_out, first_in, second_out, second_in, act, acc, zin, fin, yin, xt,
+                    load_sem, tok_send, tok_recv, send_sem, recv_sem, late_sem, gather_sem, lead_sem, store_sem, z_sem, fin_sem):
     tp = lax.axis_index("tp")
     dp = lax.axis_index("dp")
     core = lax.rem(dp, 2)
@@ -85,10 +85,6 @@
             rows[arr, pl.ds(mb * 128 + 16 * pair, 16), :] = jnp.concatenate([lo, hi], axis=0).astype(jnp.bfloat16)
 
     acc[...] = jnp.zeros_like(acc)
-    tokens_in(0, 0)
-    tokens_in(1, 0)
-    for cp in weight_loads:
-        cp.wait()
 
     n_iter = tiles
 
@@ -147,18 +143,64 @@
             into = act.at[0, :, pl.ds(0, 32 << (stage - 3)), :]
         pltpu.make_async_copy(into, into, arrival(stage, i)).wait()
 
+    def gate_up_partials(i, h):
+        u, mb, t = unit(i, h)
+        slot = lax.rem(i, SLOTS)
+        cols = pl.ds(pl.multiple_of(t * LANES, LANES), LANES)
+        r = pl.ds(pl.multiple_of(mb * 128, 128), 128)
+        pair = jnp.concatenate([wg[:, cols], wu[:, cols]], axis=1)
+        ab = dot_f32(rows[0, r, :], pair)
+        part[slot, h, 0] = ab[:, :LANES]
+        part[slot, h, 1] = ab[:, LANES:]
+
+    def down_partials(i, h):
+        u, mb, t = unit(i, h)
+        cols = pl.ds(pl.multiple_of(t * LANES, LANES), LANES)
+        r = pl.ds(pl.multiple_of(mb * 128, 128), 128)
+        part[lax.rem(i, SLOTS), h, 2] = dot_t(rows[1, r, :], wd[cols, :])
+
     def stage_partials(i):
         for h in range(2):
-            u, mb, t = unit(i, h)
-            slot = lax.rem(i, SLOTS)
-            cols = pl.ds(pl.multiple_of(t * LANES, LANES), LANES)
-            r = pl.ds(pl.multiple_of(mb * 128, 128), 128)
-            pair = jnp.concatenate([wg[:, cols], wu[:, cols]], axis=1)
-            ab = dot_f32(rows[0, r, :], pair)
-            part[slot, h, 0] = ab[:, :LANES]
-            part[slot, h, 1] = ab[:, LANES:]
-            part[slot, h, 2] = dot_t(rows[1, r, :], wd[cols, :])
+            gate_up_partials(i, h)
+            down_partials(i, h)
         start_pair(0, i)
+
+    def lead_in():
+        kinds = (pl.ds(0, 2), pl.ds(2, 1))
+
+        def to_core(k):
+            for h in range(2):
+                pltpu.make_async_remote_copy(
+                    src_ref=part.at[0, h, kinds[k], pl.ds(send_core, 64), :], dst_ref=core_in.at[h, kinds[k]],
+                    send_sem=lead_sem.at[0, k], recv_sem=lead_sem.at[1, k], device_id=core_peer, device_id_type=MESH).start()
+
+        def to_first(k):
+            both = core_in.at[pl.ds(0, 2), kinds[k]]
+            for way in range(2):
+                pltpu.make_async_copy(both, both, lead_sem.at[way, k]).wait()
+            for h in range(2):
+                o = (1 - pos1[h]) * 32
+                first_out[0, h, kinds[k]] = (part[0, h, kinds[k], pl.ds(off(core * 64 + o), 32), :]
+                                             + core_in[h, kinds[k], pl.ds(off(o), 32), :])
+                pltpu.make_async_remote_copy(
+                    src_ref=first_out.at[0, h, kinds[k]], dst_ref=first_in.at[h, kinds[k]], send_sem=send_sem.at[1, 0],
+                    recv_sem=arrival(1, 0), device_id=peer1[h], device_id_type=MESH).start()
+
+        tokens_in(0, 0)
+        for cp in weight_loads[:2]:
+            cp.wait()
+        for h in range(2):
+            gate_up_partials(0, h)
+        to_core(0)
+        tokens_in(1, 0)
+        weight_loads[2].wait()
+        for h in range(2):
+            down_partials(0, h)
+        to_core(1)
+        to_first(0)
+        for i in range(1, STARTS[1]):
+            stage_partials(i)
+        to_first(1)
 
     def stage_first(i):
         slot = lax.rem(i, SLOTS)
@@ -212,12 +254,11 @@
             u, mb, t = unit(i, h)
             cols = pl.ds(pl.multiple_of(t * LANES, LANES), LANES)
             r = pl.ds(pl.multiple_of(mb * 128, 128), 128)
+            pltpu.make_async_copy(act.at[t, :, r, :], act_hbm.at[t, :, r, :], store_sem.at[0]).start()
             add_to(0, mb, dot_f32(act[t, 0, r, :], wd[cols, :]))
             grads = jnp.concatenate([act[t, 1, r, :], act[t, 2, r, :]], axis=1)
             pair = jnp.concatenate([wg[:, cols], wu[:, cols]], axis=1)
             add_to(1, mb, dot_t(grads, pair))
-
-            pltpu.make_async_copy(act.at[t, :, r, :], act_hbm.at[t, :, r, :], store_sem.at[0]).start()
 
     z_copy = pltpu.make_async_remote_copy(
         src_ref=acc.at[:, pl.ds(0, 8), 1 - tp], dst_ref=zin, send_sem=z_sem.at[0], recv_sem=z_sem.at[1],
@@ -240,11 +281,20 @@
                 device_id=dest, device_id_type=MESH).start()
         yin[:, :, my_cols] = fin[dp]
 
+    firsts = [pltpu.make_async_copy(yin.at[k], ref, store_sem.at[4 + k]) for k, ref in enumerate((y_hbm, dx_hbm))]
+
+    def store_first():
+        blocks = fin.at[pl.ds(0, 7)]
+        for k in range(2):
+            pltpu.make_async_copy(blocks, blocks, fin_sem.at[k]).wait()
+        for cp in firsts:
+            cp.start()
+
     z_start = (tiles - 1) // 2 + STARTS[6] + DEFER + 1
 
     def forwarded(j):
         ready = jnp.maximum(j - STARTS[4] + 1, 0)
-        late = jnp.maximum(j - STARTS[4] + 1 - DEFER, 0) + jnp.maximum(j - n_iter + 1, 0)
+        late = jnp.maximum(j - STARTS[4] + 1 - DEFER, 0) + jnp.maximum(j - n_iter - STARTS[1] + 2, 0)
         return jnp.minimum(n_iter, jnp.minimum(ready, late))
 
     def run_late(j, fn):
@@ -254,14 +304,17 @@
 
         lax.fori_loop(forwarded(j - 1), forwarded(j), step, 0)
 
+    row_stores = [pltpu.make_async_copy(xt, xt_hbm, store_sem.at[1]), pltpu.make_async_copy(rows.at[1], dy_rows_hbm, store_sem.at[6])]
+
     def body(j, carry):
         pl.when(j == z_start)(z_copy.start)
-        pl.when(j == z_start + 5)(finish_first)
-        pl.when(j == n_iter + 4)(send_first)
+        pl.when(j == n_iter + STARTS[3] - 2)(finish_first)
+        pl.when(j == n_iter + STARTS[3] - 1)(send_first)
+        pl.when(j == n_iter + STARTS[6] - 2)(store_first)
 
         def run(stage, fn):
             i = j - STARTS[stage]
-            pl.when(jnp.logical_and(i >= 0, i < n_iter))(functools.partial(fn, i))
+            pl.when(jnp.logical_and(i >= (1 if stage == 1 else 0), i < n_iter))(functools.partial(fn, i))
 
         run(3, stage_act)
         run(2, stage_second)
@@ -273,28 +326,26 @@
         def _():
             tokens_in(0, 1)
             tokens_in(1, 1)
-            pltpu.make_async_copy(rows, tok_hbm, store_sem.at[1]).start()
+            xt[...] = rows[0].T
+            for cp in row_stores:
+                cp.start()
 
         run(0, stage_partials)
         run_late(j - LAGS[4] - LAGS[5], stage_outputs)
         return carry
 
-    lax.fori_loop(0, n_iter + STARTS[6], body, 0)
+    lead_in()
+    lax.fori_loop(STARTS[1], n_iter + STARTS[6], body, 0)
 
     sums = [pltpu.make_async_copy(acc.at[arr, pl.ds(8, 8)], sum_hbm.at[:, :, arr], store_sem.at[2 + arr]) for arr in range(2)]
     for cp in sums:
-        cp.start()
-    blocks = fin.at[pl.ds(0, 7)]
-    for k in range(2):
-        pltpu.make_async_copy(blocks, blocks, fin_sem.at[k]).wait()
-    firsts = [pltpu.make_async_copy(yin.at[k], ref, store_sem.at[4 + k]) for k, ref in enumerate((y_hbm, dx_hbm))]
-    for cp in firsts:
         cp.start()
     for mb in range(2):
         for arr in range(2):
             part15 = tok.at[arr, mb, pl.ds(0, 15)]
             pltpu.make_async_copy(part15, part15, tok_send.at[arr, mb]).wait()
-    pltpu.make_async_copy(rows, tok_hbm, store_sem.at[1]).wait()
+    for cp in row_stores:
+        cp.wait()
     pltpu.make_async_copy(act, act_hbm, store_sem.at[0]).wait()
     sent = act.at[:, :, pl.ds(0, 224), :]
     pltpu.make_async_copy(sent, sent, gather_sem.at[0]).wait()
@@ -310,11 +361,12 @@
     return pl.pallas_call(
         functools.partial(exchange_kernel, tiles),
         out_shape=(jax.ShapeDtypeStruct((tiles, 3, 256, LANES), bf16),
-                   jax.ShapeDtypeStruct((2, 256, d_loc), bf16),
+                   jax.ShapeDtypeStruct((d_loc, 256), bf16),
+                   jax.ShapeDtypeStruct((256, d_loc), bf16),
                    jax.ShapeDtypeStruct((8, 2, 2, 8, d_loc), f32),
                    *[jax.ShapeDtypeStruct((8, 4096), bf16)] * 2),
         in_specs=[any_spec] * 5,
-        out_specs=(any_spec,) * 5,
+        out_specs=(any_spec,) * 6,
         scratch_shapes=[
             pltpu.VMEM((2, 2, 8, 4096), bf16),
             pltpu.VMEM((2, 2, 16, 8, d_loc), bf16),
@@ -333,6 +385,7 @@
             pltpu.VMEM((2, 8, 8, d_loc), f32),
             pltpu.VMEM((8, 2, 8, d_loc), bf16),
             pltpu.VMEM((2, 8, 4096), bf16),
+            pltpu.VMEM((d_loc, 256), bf16),
             pltpu.SemaphoreType.DMA((5,)),
             pltpu.SemaphoreType.DMA((2, 2)),
             pltpu.SemaphoreType.DMA((2, 2)),
@@ -340,7 +393,8 @@
             pltpu.SemaphoreType.DMA((3, SLOTS)),
             pltpu.SemaphoreType.DMA((3, LATE_SLOTS)),
             pltpu.SemaphoreType.DMA((1,)),
-            pltpu.SemaphoreType.DMA((6,)),
+            pltpu.SemaphoreType.DMA((2, 2)),
+            pltpu.SemaphoreType.DMA((7,)),
             pltpu.SemaphoreType.DMA((2,)),
             pltpu.SemaphoreType.DMA((2,)),
         ],
@@ -354,10 +408,11 @@
 WIDTH = 2 * LANES
 
 
-def grads_kernel(tiles, tok_hbm, act_hbm, dg_hbm, du_hbm, dd_hbm, tok, xt, act, gate, up, down, load_sem, out_sem):
+def grads_kernel(tiles, xt_hbm, dy_hbm, act_hbm, dg_hbm, du_hbm, dd_hbm, xt, dy, act, gate, up, down, load_sem, out_sem):
     pairs = tiles // 2
-    tok_copy = pltpu.make_async_copy(tok_hbm, tok, load_sem.at[pairs + 1])
-    tok_copy.start()
+    row_loads = [pltpu.make_async_copy(xt_hbm, xt, load_sem.at[pairs + 1]), pltpu.make_async_copy(dy_hbm, dy, load_sem.at[pairs + 2])]
+    for cp in row_loads:
+        cp.start()
 
     def act_copy(i, n):
         span = pl.ds(2 * i, n)
@@ -367,8 +422,8 @@
         act_copy(i, 2).start()
     if tiles % 2:
         act_copy(pairs, 1).start()
-    tok_copy.wait()
-    xt[...] = tok[0].T
+    for cp in row_loads:
+        cp.wait()
 
     def out_copies(i, slot, width):
         cols = pl.ds(pl.multiple_of(i * WIDTH, WIDTH), width)
@@ -393,7 +448,7 @@
         part = slice(0, n * LANES)
         gate[slot, :, part] = dot_f32(xt[...], cols(1))
         up[slot, :, part] = dot_f32(xt[...], cols(2))
-        down[slot, part, :] = lax.dot_general(cols(0), tok[1], TRANS_A, preferred_element_type=jnp.float32)
+        down[slot, part, :] = lax.dot_general(cols(0), dy[...], TRANS_A, preferred_element_type=jnp.float32)
         for cp in out_copies(i, slot, n * LANES):
             cp.start()
 
@@ -411,29 +466,29 @@
             cp.wait()
 
 
-def weight_grads(tok, act):
+def weight_grads(xt, dy_rows, act):
     tiles = act.shape[0]
-    d_loc = tok.shape[-1]
+    d_loc = xt.shape[0]
     f_loc = tiles * LANES
     any_spec = pl.BlockSpec(memory_space=pl.ANY)
     f32, bf16 = jnp.float32, jnp.bfloat16
     return pl.pallas_call(
-        functools.partial(grads_kernel, tiles), in_specs=[any_spec] * 2, out_specs=[any_spec] * 3,
+        functools.partial(grads_kernel, tiles), in_specs=[any_spec] * 3, out_specs=[any_spec] * 3,
         out_shape=[jax.ShapeDtypeStruct((d_loc, f_loc), f32)] * 2 + [jax.ShapeDtypeStruct((f_loc, d_loc), f32)],
         scratch_shapes=[
-            pltpu.VMEM((2, 256, d_loc), bf16),
             pltpu.VMEM((d_loc, 256), bf16),
+            pltpu.VMEM((256, d_loc), bf16),
             pltpu.VMEM(act.shape, bf16),
             pltpu.VMEM((OUT_SLOTS, d_loc, WIDTH), f32),
             pltpu.VMEM((OUT_SLOTS, d_loc, WIDTH), f32),
             pltpu.VMEM((OUT_SLOTS, WIDTH, d_loc), f32),
-            pltpu.SemaphoreType.DMA((tiles // 2 + 2,)),
+            pltpu.SemaphoreType.DMA((tiles // 2 + 3,)),
             pltpu.SemaphoreType.DMA((3, OUT_SLOTS)),
         ],
         compiler_params=pltpu.CompilerParams(vmem_limit_bytes=62 * 2**20),
         cost_estimate=pl.CostEstimate(flops=6 * 256 * d_loc * f_loc, bytes_accessed=44 * 10**6, transcendentals=0),
         name="weight_grads",
-    )(tok, act)
+    )(xt, dy_rows, act)
 
 
 def solution(mesh):
@@ -442,13 +497,13 @@
     out_specs = (row_spec, row_spec, P("dp", "tp"), P("dp", "tp"), P("tp", "dp"))
 
     def local_step(x_loc, w_gate, w_up, w_down, dy_loc):
-        act, tok, part, y_first, dx_first = exchange(x_loc, dy_loc, w_gate, w_up, w_down)
+        act, xt, dy_rows, part, y_first, dx_first = exchange(x_loc, dy_loc, w_gate, w_up, w_down)
         part = lax.all_to_all(part.reshape(16, 2, 8, -1), ("dp", "tp"), split_axis=0, concat_axis=0, tiled=True)
         part = part.reshape(8, 2, 2, 8, -1)
         out = (part[:, 0] + part[:, 1]).transpose(1, 2, 0, 3).reshape(2, 8, 4096)
         y = jnp.stack([y_first, (x_loc[1].astype(jnp.float32) + out[0]).astype(jnp.bfloat16)])
         dx = jnp.stack([dx_first, (dy_loc[1].astype(jnp.float32) + out[1]).astype(jnp.bfloat16)])
-        dg, du, dd = weight_grads(tok, act)
+        dg, du, dd = weight_grads(xt, dy_rows, act)
         return y, dx, dg, du, dd
 
     return jax.shard_map(local_step, mesh=mesh, in_specs=in_specs, out_specs=out_specs, check_vma=False)

time: 141 us -> 139 us (0.986)
  Pallas kernels: 137 us -> 135 us
    pallas_call x1, Pallas kernels: 123 us -> 121 us  [exchange(): pl.pallas_call(functools.partial(exchange_kernel, tiles), out_shape=(jax....]
where the time goes in v5:
time: 139 us
  Pallas kernels  135 us (97%)
  starting transfers between devices  2.33 us (2%)
    pallas_call x1, Pallas kernels, exchange(): pl.pallas_call(functools.partial(exchange_kernel, tiles), out_shape=(jax....  121 us
    pallas_call x1, Pallas kernels, weight_grads(): pl.pallas_call(functools.partial(grads_kernel, tiles), in_specs=[any_spec...  13.7 us
  transfers between devices with their start and end apart: 1, of which 0 were waited for; matrix products, arithmetic and copies ran while one was open for 0% of the time, Pallas kernels for 10%

profile of v5, /device:TPU:0, one launch (start us, length us, event | category | flops | bytes accessed | tf_op | source)
XLA Modules:
  0.0 138.5 jit_solution(7301498639878823281)
XLA Ops:
  0.6 120.9 %exchange.1 = (bf16[43,3,256,128]{3,2,1,0:T(8,128)(2,1)}, bf16[512,256]{1,0:T(8,128)(2,1)}, bf16[256,512]{1,0:T(8,128)(2,1)}, f32[8,2,2,8,512]{4,3,2,1,0:T(8,128...) custom-call(bf16[2,8,4096]{2,1,0:T(8,128)(2,1)} %x_hbm.1, bf16[2,8,4096]{2,1,0:T(8,128)(2,1)} %dy_hbm.1, ...), custom_call_target="tpu_custom_call" | custom-call | flops 8999999488 | bytes 28000000 | tf_op jit(solution)/shard_map/exchange/pallas_call | solution.py:361
  121.6 2.3 %all-to-all-start = ((f32[16,2,8,512]{3,2,1,0:T(8,128)}), f32[16,2,8,512]{3,2,1,0:T(8,128)S(1)}, u32[]{:S(2)}, u32[]{:S(2)}) async-start(f32[16,2,8,512]{3,2,1,0:T(8,128)} %bitcast.11), calls=%async_computation | async-start | bytes 1048576 | tf_op jit(solution)/shard_map/all_to_all | solution.py:501
  123.9 0.0 copy-start.2
  123.9 0.0 copy-start.3
  123.9 0.0 copy-start
  124.0 0.0 copy-start.1
  124.0 13.7 %weight_grads.1 = (f32[512,5504]{1,0:T(8,128)}, f32[512,5504]{1,0:T(8,128)}, f32[5504,512]{1,0:T(8,128)}) custom-call(bf16[512,256]{1,0:T(8,128)(2,1)} %get-tuple-element.17.xt_hbm, bf16[256,512]{1,0:T(8,128)(2,1)} %get-tuple-element.18.dy_hbm, bf16[43,3,256,128]{3,2,1,0:T(8,128)(2,1)} %get-tuple-element.19.act_hbm), custom_call_target="tpu_custom_call" | custom-call | flops 4328521728 | bytes 44000000 | tf_op jit(solution)/shard_map/weight_grads/pallas_call | solution.py:475
  137.6 0.0 all-to-all-done
  137.7 0.0 copy-done.2
  137.7 0.0 copy-done.3
  137.8 0.0 copy-done
  137.8 0.0 copy-done.1
  137.8 0.7 pad_maximum_fusion
  (4 shorter events, 0.1 us)
Async XLA Ops:
  121.6 16.0 %all-to-all-start = ((f32[16,2,8,512]{3,2,1,0:T(8,128)}), f32[16,2,8,512]{3,2,1,0:T(8,128)S(1)}, u32[]{:S(2)}, u32[]{:S(2)}) async-start(f32[16,2,8,512]{3,2,1,0:T(8,128)} %bitcast.11), calls=%async_computation | async-start | bytes 1048576 | tf_op jit(solution)/shard_map/all_to_all | solution.py:501
  123.9 13.8 %copy-start.2 = (bf16[2,8,4096]{2,1,0:T(8,128)(2,1)S(1)}, bf16[2,8,4096]{2,1,0:T(8,128)(2,1)}, u32[]{:S(2)}) copy-start(bf16[2,8,4096]{2,1,0:T(8,128)(2,1)} %dy_hbm.1) | copy-start | bytes 393220
  123.9 13.8 %copy-start.3 = (bf16[2,8,4096]{2,1,0:T(8,128)(2,1)S(1)}, bf16[2,8,4096]{2,1,0:T(8,128)(2,1)}, u32[]{:S(2)}) copy-start(bf16[2,8,4096]{2,1,0:T(8,128)(2,1)} %x_hbm.1) | copy-start | bytes 393220
  123.9 13.8 %copy-start = (bf16[8,4096]{1,0:T(8,128)(2,1)S(1)}, bf16[8,4096]{1,0:T(8,128)(2,1)}, u32[]{:S(2)}) copy-start(bf16[8,4096]{1,0:T(8,128)(2,1)} %get-tuple-element.14) | copy-start | bytes 196612
  124.0 13.8 %copy-start.1 = (bf16[8,4096]{1,0:T(8,128)(2,1)S(1)}, bf16[8,4096]{1,0:T(8,128)(2,1)}, u32[]{:S(2)}) copy-start(bf16[8,4096]{1,0:T(8,128)(2,1)} %get-tuple-element.16) | copy-start | bytes 196612

commit v6 on v5

--- a/solution.py
+++ b/solution.py
@@ -10,8 +10,8 @@
 MESH = pl.DeviceIdType.MESH
 LANES = 128
 SLOTS = 8
-LATE_SLOTS = 16
-DEFER = 8
+LATE_SLOTS = 12
+DEFER = 6
 LAGS = (3, 3, 2, 2, 2, 1)
 STARTS = tuple(sum(LAGS[:k]) for k in range(len(LAGS) + 1))
 TRANS_B = (((1,), (1,)), ((), ()))
@@ -29,13 +29,13 @@
 def exchange_kernel(tiles, x_hbm, dy_hbm, wg_hbm, wu_hbm, wd_hbm,
                     act_hbm, xt_hbm, dy_rows_hbm, sum_hbm, y_hbm, dx_hbm,
                     loc, tok, rows, wg, wu, wd, part, core_in, first_out, first_in, second_out, second_in, act, acc, zin, fin, yin, xt,
-                    load_sem, tok_send, tok_recv, send_sem, recv_sem, late_sem, gather_sem, lead_sem, store_sem, z_sem, fin_sem):
+                    load_sem, tok_send, tok_recv, send_sem, recv_sem, late_sem, gather_sem, lead_sem, plane_sem, store_sem, z_sem, fin_sem):
     tp = lax.axis_index("tp")
     dp = lax.axis_index("dp")
     core = lax.rem(dp, 2)
     xpos = lax.rem(lax.div(dp, 2), 2)
     ypos = lax.div(dp, 4)
-    me = dp * 2 + tp
+    me = tp * 8 + dp
 
     def device(fc, fx, fy, fz):
         dc = 1 - core if fc else core
@@ -63,9 +63,10 @@
         cp.wait()
     pl.semaphore_wait(barrier, 15)
 
+    plane = [flags for flags in others if not flags[3]]
     for mb in range(2):
         for arr in range(2):
-            for flags in others:
+            for flags in (plane if mb else others):
                 dest = device(*flags)
                 pltpu.make_async_remote_copy(
                     src_ref=loc.at[arr, mb, :, pl.ds(pl.multiple_of(dest[1] * 512, 512), 512)],
@@ -76,12 +77,27 @@
         for arr in range(2):
             tok[arr, mb, me] = loc[arr, mb, :, pl.ds(pl.multiple_of(dp * 512, 512), 512)]
 
+    def plane_copy(arr):
+        slab = tok.at[arr, 1, pl.ds(pl.multiple_of(8 * tp, 8), 8)]
+        return pltpu.make_async_remote_copy(
+            src_ref=slab, dst_ref=slab, send_sem=plane_sem.at[0, arr], recv_sem=plane_sem.at[1, arr],
+            device_id=device(0, 0, 0, 1), device_id_type=MESH)
+
+    def send_plane():
+        for arr in range(2):
+            got = tok.at[arr, 1, pl.ds(0, 7)]
+            pltpu.make_async_copy(got, got, tok_recv.at[arr, 1]).wait()
+            plane_copy(arr).start()
+
     def tokens_in(arr, mb):
-        part15 = tok.at[arr, mb, pl.ds(0, 15)]
-        pltpu.make_async_copy(part15, part15, tok_recv.at[arr, mb]).wait()
+        if mb:
+            plane_copy(arr).wait()
+        else:
+            part15 = tok.at[arr, 0, pl.ds(0, 15)]
+            pltpu.make_async_copy(part15, part15, tok_recv.at[arr, 0]).wait()
         for pair in range(8):
-            lo = tok[arr, mb, 2 * pair].astype(jnp.float32)
-            hi = tok[arr, mb, 2 * pair + 1].astype(jnp.float32)
+            lo = tok[arr, mb, pair].astype(jnp.float32)
+            hi = tok[arr, mb, 8 + pair].astype(jnp.float32)
             rows[arr, pl.ds(mb * 128 + 16 * pair, 16), :] = jnp.concatenate([lo, hi], axis=0).astype(jnp.bfloat16)
 
     acc[...] = jnp.zeros_like(acc)
@@ -263,7 +279,6 @@
     z_copy = pltpu.make_async_remote_copy(
         src_ref=acc.at[:, pl.ds(0, 8), 1 - tp], dst_ref=zin, send_sem=z_sem.at[0], recv_sem=z_sem.at[1],
         device_id=device(0, 0, 0, 1), device_id_type=MESH)
-    plane = [flags for flags in others if not flags[3]]
     my_cols = pl.ds(pl.multiple_of(dp * 512, 512), 512)
 
     def finish_first():
@@ -271,7 +286,7 @@
         for arr in range(2):
             for blk in range(8):
                 total = acc[arr, blk, tp] + zin[arr, blk]
-                fin[blk, arr] = (tok[arr, 0, 2 * blk + tp].astype(jnp.float32) + total).astype(jnp.bfloat16)
+                fin[blk, arr] = (tok[arr, 0, 8 * tp + blk].astype(jnp.float32) + total).astype(jnp.bfloat16)
 
     def send_first():
         for flags in plane:
@@ -307,19 +322,19 @@
     row_stores = [pltpu.make_async_copy(xt, xt_hbm, store_sem.at[1]), pltpu.make_async_copy(rows.at[1], dy_rows_hbm, store_sem.at[6])]
 
     def body(j, carry):
+        pl.when(j == STARTS[1] + 4)(send_plane)
         pl.when(j == z_start)(z_copy.start)
         pl.when(j == n_iter + STARTS[3] - 2)(finish_first)
-        pl.when(j == n_iter + STARTS[3] - 1)(send_first)
-        pl.when(j == n_iter + STARTS[6] - 2)(store_first)
 
         def run(stage, fn):
             i = j - STARTS[stage]
             pl.when(jnp.logical_and(i >= (1 if stage == 1 else 0), i < n_iter))(functools.partial(fn, i))
 
+        run(1, stage_first)
+        run(2, stage_second)
         run(3, stage_act)
-        run(2, stage_second)
-        run(1, stage_first)
         run_late(j, functools.partial(stage_forward, 4))
+        pl.when(j == n_iter + STARTS[4] - 1)(send_first)
         run_late(j - LAGS[4], functools.partial(stage_forward, 5))
 
         @pl.when(j == tiles // 2 - 2)
@@ -340,10 +355,11 @@
     sums = [pltpu.make_async_copy(acc.at[arr, pl.ds(8, 8)], sum_hbm.at[:, :, arr], store_sem.at[2 + arr]) for arr in range(2)]
     for cp in sums:
         cp.start()
+    store_first()
     for mb in range(2):
         for arr in range(2):
-            part15 = tok.at[arr, mb, pl.ds(0, 15)]
-            pltpu.make_async_copy(part15, part15, tok_send.at[arr, mb]).wait()
+            sent = tok.at[arr, mb, pl.ds(0, 7 if mb else 15)]
+            pltpu.make_async_copy(sent, sent, tok_send.at[arr, mb]).wait()
     for cp in row_stores:
         cp.wait()
     pltpu.make_async_copy(act, act_hbm, store_sem.at[0]).wait()
@@ -394,6 +410,7 @@
             pltpu.SemaphoreType.DMA((3, LATE_SLOTS)),
             pltpu.SemaphoreType.DMA((1,)),
             pltpu.SemaphoreType.DMA((2, 2)),
+            pltpu.SemaphoreType.DMA((2, 2)),
             pltpu.SemaphoreType.DMA((7,)),
             pltpu.SemaphoreType.DMA((2,)),
             pltpu.SemaphoreType.DMA((2,)),

time: 139 us -> 138 us (level)
  no operation moved by 1% of the time
where the time goes in v6:
time: 138 us
  Pallas kernels  134 us (97%)
  starting transfers between devices  2.33 us (2%)
    pallas_call x1, Pallas kernels, exchange(): pl.pallas_call(functools.partial(exchange_kernel, tiles), out_shape=(jax....  120 us
    pallas_call x1, Pallas kernels, weight_grads(): pl.pallas_call(functools.partial(grads_kernel, tiles), in_specs=[any_spec...  13.7 us
  transfers between devices with their start and end apart: 1, of which 0 were waited for; matrix products, arithmetic and copies ran while one was open for 0% of the time, Pallas kernels for 10%

profile of v6, /device:TPU:0, one launch (start us, length us, event | category | flops | bytes accessed | tf_op | source)
XLA Modules:
  0.0 137.6 jit_solution(7251307639802294550)
XLA Ops:
  0.6 120.0 %exchange.1 = (bf16[43,3,256,128]{3,2,1,0:T(8,128)(2,1)}, bf16[512,256]{1,0:T(8,128)(2,1)}, bf16[256,512]{1,0:T(8,128)(2,1)}, f32[8,2,2,8,512]{4,3,2,1,0:T(8,128...) custom-call(bf16[2,8,4096]{2,1,0:T(8,128)(2,1)} %x_hbm.1, bf16[2,8,4096]{2,1,0:T(8,128)(2,1)} %dy_hbm.1, ...), custom_call_target="tpu_custom_call" | custom-call | flops 8999999488 | bytes 28000000 | tf_op jit(solution)/shard_map/exchange/pallas_call | solution.py:377
  120.7 2.3 %all-to-all-start = ((f32[16,2,8,512]{3,2,1,0:T(8,128)}), f32[16,2,8,512]{3,2,1,0:T(8,128)S(1)}, u32[]{:S(2)}, u32[]{:S(2)}) async-start(f32[16,2,8,512]{3,2,1,0:T(8,128)} %bitcast.11), calls=%async_computation | async-start | bytes 1048576 | tf_op jit(solution)/shard_map/all_to_all | solution.py:518
  123.0 0.0 copy-start.2
  123.0 0.0 copy-start.3
  123.0 0.0 copy-start
  123.0 0.0 copy-start.1
  123.1 13.7 %weight_grads.1 = (f32[512,5504]{1,0:T(8,128)}, f32[512,5504]{1,0:T(8,128)}, f32[5504,512]{1,0:T(8,128)}) custom-call(bf16[512,256]{1,0:T(8,128)(2,1)} %get-tuple-element.17.xt_hbm, bf16[256,512]{1,0:T(8,128)(2,1)} %get-tuple-element.18.dy_hbm, bf16[43,3,256,128]{3,2,1,0:T(8,128)(2,1)} %get-tuple-element.19.act_hbm), custom_call_target="tpu_custom_call" | custom-call | flops 4328521728 | bytes 44000000 | tf_op jit(solution)/shard_map/weight_grads/pallas_call | solution.py:492
  136.7 0.0 all-to-all-done
  136.8 0.0 copy-done.2
  136.8 0.0 copy-done.3
  136.9 0.0 copy-done
  136.9 0.0 copy-done.1
  136.9 0.7 pad_maximum_fusion
  (4 shorter events, 0.1 us)
Async XLA Ops:
  120.7 16.0 %all-to-all-start = ((f32[16,2,8,512]{3,2,1,0:T(8,128)}), f32[16,2,8,512]{3,2,1,0:T(8,128)S(1)}, u32[]{:S(2)}, u32[]{:S(2)}) async-start(f32[16,2,8,512]{3,2,1,0:T(8,128)} %bitcast.11), calls=%async_computation | async-start | bytes 1048576 | tf_op jit(solution)/shard_map/all_to_all | solution.py:518
  123.0 13.8 %copy-start.2 = (bf16[2,8,4096]{2,1,0:T(8,128)(2,1)S(1)}, bf16[2,8,4096]{2,1,0:T(8,128)(2,1)}, u32[]{:S(2)}) copy-start(bf16[2,8,4096]{2,1,0:T(8,128)(2,1)} %dy_hbm.1) | copy-start | bytes 393220
  123.0 13.8 %copy-start.3 = (bf16[2,8,4096]{2,1,0:T(8,128)(2,1)S(1)}, bf16[2,8,4096]{2,1,0:T(8,128)(2,1)}, u32[]{:S(2)}) copy-start(bf16[2,8,4096]{2,1,0:T(8,128)(2,1)} %x_hbm.1) | copy-start | bytes 393220
  123.0 13.8 %copy-start = (bf16[8,4096]{1,0:T(8,128)(2,1)S(1)}, bf16[8,4096]{1,0:T(8,128)(2,1)}, u32[]{:S(2)}) copy-start(bf16[8,4096]{1,0:T(8,128)(2,1)} %get-tuple-element.14) | copy-start | bytes 196612
  123.0 13.8 %copy-start.1 = (bf16[8,4096]{1,0:T(8,128)(2,1)S(1)}, bf16[8,4096]{1,0:T(8,128)(2,1)}, u32[]{:S(2)}) copy-start(bf16[8,4096]{1,0:T(8,128)(2,1)} %get-tuple-element.16) | copy-start | bytes 196612

commit v7 on v6

--- a/solution.py
+++ b/solution.py
@@ -12,6 +12,7 @@
 SLOTS = 8
 LATE_SLOTS = 12
 DEFER = 6
+LEAD = 2
 LAGS = (3, 3, 2, 2, 2, 1)
 STARTS = tuple(sum(LAGS[:k]) for k in range(len(LAGS) + 1))
 TRANS_B = (((1,), (1,)), ((), ()))
@@ -59,13 +60,13 @@
     barrier = pltpu.get_barrier_semaphore()
     for flags in others:
         pl.semaphore_signal(barrier, 1, device_id=device(*flags), device_id_type=MESH)
-    for cp in token_loads:
-        cp.wait()
     pl.semaphore_wait(barrier, 15)
 
     plane = [flags for flags in others if not flags[3]]
     for mb in range(2):
         for arr in range(2):
+            if mb == 0:
+                token_loads[arr].wait()
             for flags in (plane if mb else others):
                 dest = device(*flags)
                 pltpu.make_async_remote_copy(
@@ -139,7 +140,7 @@
             src = dst = act.at[t, :, pl.ds(off(base), 64), :]
             dev = core_peer
         return pltpu.make_async_remote_copy(
-            src_ref=src, dst_ref=dst, send_sem=send_sem.at[stage, slot] if stage < 3 else gather_sem.at[0],
+            src_ref=src, dst_ref=dst, send_sem=send_sem.at[stage, lax.rem(i, 4)] if stage < 3 else gather_sem.at[0],
             recv_sem=arrival(stage, i), device_id=dev, device_id_type=MESH)
 
     def arrival(stage, i):
@@ -154,7 +155,7 @@
     def wait_pair(stage, i):
         if stage < 3:
             into = (core_in, first_in, second_in)[stage].at[pl.ds(2 * i, 2)]
-            pltpu.make_async_copy(into, into, send_sem.at[stage, lax.rem(i, SLOTS)]).wait()
+            pltpu.make_async_copy(into, into, send_sem.at[stage, lax.rem(i, 4)]).wait()
         else:
             into = act.at[0, :, pl.ds(0, 32 << (stage - 3)), :]
         pltpu.make_async_copy(into, into, arrival(stage, i)).wait()
@@ -184,39 +185,43 @@
     def lead_in():
         kinds = (pl.ds(0, 2), pl.ds(2, 1))
 
-        def to_core(k):
+        def to_core(i, k):
             for h in range(2):
                 pltpu.make_async_remote_copy(
-                    src_ref=part.at[0, h, kinds[k], pl.ds(send_core, 64), :], dst_ref=core_in.at[h, kinds[k]],
-                    send_sem=lead_sem.at[0, k], recv_sem=lead_sem.at[1, k], device_id=core_peer, device_id_type=MESH).start()
-
-        def to_first(k):
-            both = core_in.at[pl.ds(0, 2), kinds[k]]
+                    src_ref=part.at[i, h, kinds[k], pl.ds(send_core, 64), :], dst_ref=core_in.at[2 * i + h, kinds[k]],
+                    send_sem=lead_sem.at[0, k, i], recv_sem=lead_sem.at[1, k, i], device_id=core_peer, device_id_type=MESH).start()
+
+        def to_first(i, k):
+            both = core_in.at[pl.ds(2 * i, 2), kinds[k]]
             for way in range(2):
-                pltpu.make_async_copy(both, both, lead_sem.at[way, k]).wait()
+                pltpu.make_async_copy(both, both, lead_sem.at[way, k, i]).wait()
             for h in range(2):
                 o = (1 - pos1[h]) * 32
-                first_out[0, h, kinds[k]] = (part[0, h, kinds[k], pl.ds(off(core * 64 + o), 32), :]
-                                             + core_in[h, kinds[k], pl.ds(off(o), 32), :])
+                first_out[i, h, kinds[k]] = (part[i, h, kinds[k], pl.ds(off(core * 64 + o), 32), :]
+                                             + core_in[2 * i + h, kinds[k], pl.ds(off(o), 32), :])
                 pltpu.make_async_remote_copy(
-                    src_ref=first_out.at[0, h, kinds[k]], dst_ref=first_in.at[h, kinds[k]], send_sem=send_sem.at[1, 0],
-                    recv_sem=arrival(1, 0), device_id=peer1[h], device_id_type=MESH).start()
+                    src_ref=first_out.at[i, h, kinds[k]], dst_ref=first_in.at[2 * i + h, kinds[k]], send_sem=send_sem.at[1, i],
+                    recv_sem=arrival(1, i), device_id=peer1[h], device_id_type=MESH).start()
 
         tokens_in(0, 0)
         for cp in weight_loads[:2]:
             cp.wait()
-        for h in range(2):
-            gate_up_partials(0, h)
-        to_core(0)
+        for i in range(LEAD):
+            for h in range(2):
+                gate_up_partials(i, h)
+            to_core(i, 0)
+        for i in range(LEAD):
+            to_first(i, 0)
         tokens_in(1, 0)
         weight_loads[2].wait()
-        for h in range(2):
-            down_partials(0, h)
-        to_core(1)
-        to_first(0)
-        for i in range(1, STARTS[1]):
+        for i in range(LEAD):
+            for h in range(2):
+                down_partials(i, h)
+            to_core(i, 1)
+        for i in range(LEAD, STARTS[1]):
             stage_partials(i)
-        to_first(1)
+        for i in range(LEAD):
+            to_first(i, 1)
 
     def stage_first(i):
         slot = lax.rem(i, SLOTS)
@@ -328,7 +333,7 @@
 
         def run(stage, fn):
             i = j - STARTS[stage]
-            pl.when(jnp.logical_and(i >= (1 if stage == 1 else 0), i < n_iter))(functools.partial(fn, i))
+            pl.when(jnp.logical_and(i >= (LEAD if stage == 1 else 0), i < n_iter))(functools.partial(fn, i))
 
         run(1, stage_first)
         run(2, stage_second)
@@ -405,11 +410,11 @@
             pltpu.SemaphoreType.DMA((5,)),
             pltpu.SemaphoreType.DMA((2, 2)),
             pltpu.SemaphoreType.DMA((2, 2)),
-            pltpu.SemaphoreType.DMA((3, SLOTS)),
+            pltpu.SemaphoreType.DMA((3, 4)),
             pltpu.SemaphoreType.DMA((3, SLOTS)),
             pltpu.SemaphoreType.DMA((3, LATE_SLOTS)),
             pltpu.SemaphoreType.DMA((1,)),
-            pltpu.SemaphoreType.DMA((2, 2)),
+            pltpu.SemaphoreType.DMA((2, 2, LEAD)),
             pltpu.SemaphoreType.DMA((2, 2)),
             pltpu.SemaphoreType.DMA((7,)),
             pltpu.SemaphoreType.DMA((2,)),

time: 138 us -> 137 us (level)
  no operation moved by 1% of the time
where the time goes in v7:
time: 137 us
  Pallas kernels  133 us (97%)
  starting transfers between devices  2.33 us (2%)
    pallas_call x1, Pallas kernels, exchange(): pl.pallas_call(functools.partial(exchange_kernel, tiles), out_shape=(jax....  119 us
    pallas_call x1, Pallas kernels, weight_grads(): pl.pallas_call(functools.partial(grads_kernel, tiles), in_specs=[any_spec...  13.7 us
  transfers between devices with their start and end apart: 1, of which 0 were waited for; matrix products, arithmetic and copies ran while one was open for 0% of the time, Pallas kernels for 10%

profile of v7, /device:TPU:0, one launch (start us, length us, event | category | flops | bytes accessed | tf_op | source)
XLA Modules:
  0.0 136.9 jit_solution(9844050663628057512)
XLA Ops:
  0.6 119.3 %exchange.1 = (bf16[43,3,256,128]{3,2,1,0:T(8,128)(2,1)}, bf16[512,256]{1,0:T(8,128)(2,1)}, bf16[256,512]{1,0:T(8,128)(2,1)}, f32[8,2,2,8,512]{4,3,2,1,0:T(8,128...) custom-call(bf16[2,8,4096]{2,1,0:T(8,128)(2,1)} %x_hbm.1, bf16[2,8,4096]{2,1,0:T(8,128)(2,1)} %dy_hbm.1, ...), custom_call_target="tpu_custom_call" | custom-call | flops 8999999488 | bytes 28000000 | tf_op jit(solution)/shard_map/exchange/pallas_call | solution.py:382
  120.0 2.3 %all-to-all-start = ((f32[16,2,8,512]{3,2,1,0:T(8,128)}), f32[16,2,8,512]{3,2,1,0:T(8,128)S(1)}, u32[]{:S(2)}, u32[]{:S(2)}) async-start(f32[16,2,8,512]{3,2,1,0:T(8,128)} %bitcast.11), calls=%async_computation | async-start | bytes 1048576 | tf_op jit(solution)/shard_map/all_to_all | solution.py:523
  122.3 0.0 copy-start.2
  122.3 0.0 copy-start.3
  122.3 0.0 copy-start
  122.3 0.0 copy-start.1
  122.3 13.7 %weight_grads.1 = (f32[512,5504]{1,0:T(8,128)}, f32[512,5504]{1,0:T(8,128)}, f32[5504,512]{1,0:T(8,128)}) custom-call(bf16[512,256]{1,0:T(8,128)(2,1)} %get-tuple-element.17.xt_hbm, bf16[256,512]{1,0:T(8,128)(2,1)} %get-tuple-element.18.dy_hbm, bf16[43,3,256,128]{3,2,1,0:T(8,128)(2,1)} %get-tuple-element.19.act_hbm), custom_call_target="tpu_custom_call" | custom-call | flops 4328521728 | bytes 44000000 | tf_op jit(solution)/shard_map/weight_grads/pallas_call | solution.py:497
  136.0 0.0 all-to-all-done
  136.1 0.0 copy-done.2
  136.1 0.0 copy-done.3
  136.2 0.0 copy-done
  136.2 0.0 copy-done.1
  136.2 0.7 pad_maximum_fusion
  (4 shorter events, 0.1 us)
Async XLA Ops:
  120.0 16.0 %all-to-all-start = ((f32[16,2,8,512]{3,2,1,0:T(8,128)}), f32[16,2,8,512]{3,2,1,0:T(8,128)S(1)}, u32[]{:S(2)}, u32[]{:S(2)}) async-start(f32[16,2,8,512]{3,2,1,0:T(8,128)} %bitcast.11), calls=%async_computation | async-start | bytes 1048576 | tf_op jit(solution)/shard_map/all_to_all | solution.py:523
  122.3 13.8 %copy-start.2 = (bf16[2,8,4096]{2,1,0:T(8,128)(2,1)S(1)}, bf16[2,8,4096]{2,1,0:T(8,128)(2,1)}, u32[]{:S(2)}) copy-start(bf16[2,8,4096]{2,1,0:T(8,128)(2,1)} %dy_hbm.1) | copy-start | bytes 393220
  122.3 13.8 %copy-start.3 = (bf16[2,8,4096]{2,1,0:T(8,128)(2,1)S(1)}, bf16[2,8,4096]{2,1,0:T(8,128)(2,1)}, u32[]{:S(2)}) copy-start(bf16[2,8,4096]{2,1,0:T(8,128)(2,1)} %x_hbm.1) | copy-start | bytes 393220
  122.3 13.8 %copy-start = (bf16[8,4096]{1,0:T(8,128)(2,1)S(1)}, bf16[8,4096]{1,0:T(8,128)(2,1)}, u32[]{:S(2)}) copy-start(bf16[8,4096]{1,0:T(8,128)(2,1)} %get-tuple-element.14) | copy-start | bytes 196612
  122.3 13.8 %copy-start.1 = (bf16[8,4096]{1,0:T(8,128)(2,1)S(1)}, bf16[8,4096]{1,0:T(8,128)(2,1)}, u32[]{:S(2)}) copy-start(bf16[8,4096]{1,0:T(8,128)(2,1)} %get-tuple-element.16) | copy-start | bytes 196612

commit v8 on v7

--- a/solution.py
+++ b/solution.py
@@ -426,24 +426,25 @@
     )(x_loc, dy_loc, w_gate, w_up, w_down)
 
 
-OUT_SLOTS = 4
+OUT_SLOTS = 3
 WIDTH = 2 * LANES
 
 
 def grads_kernel(tiles, xt_hbm, dy_hbm, act_hbm, dg_hbm, du_hbm, dd_hbm, xt, dy, act, gate, up, down, load_sem, out_sem):
     pairs = tiles // 2
-    row_loads = [pltpu.make_async_copy(xt_hbm, xt, load_sem.at[pairs + 1]), pltpu.make_async_copy(dy_hbm, dy, load_sem.at[pairs + 2])]
+    row_loads = [pltpu.make_async_copy(xt_hbm, xt, load_sem.at[10]), pltpu.make_async_copy(dy_hbm, dy, load_sem.at[11])]
     for cp in row_loads:
         cp.start()
 
-    def act_copy(i, n):
-        span = pl.ds(2 * i, n)
-        return pltpu.make_async_copy(act_hbm.at[span], act.at[span], load_sem.at[i])
-
-    for i in range(pairs):
-        act_copy(i, 2).start()
-    if tiles % 2:
-        act_copy(pairs, 1).start()
+    edges = [0, 1, 3] + list(range(7, pairs, 4)) + [pairs]
+
+    def act_copy(k):
+        last = tiles if edges[k + 1] == pairs else 2 * edges[k + 1]
+        span = pl.ds(2 * edges[k], last - 2 * edges[k])
+        return pltpu.make_async_copy(act_hbm.at[span], act.at[span], load_sem.at[k])
+
+    for k in range(len(edges) - 1):
+        act_copy(k).start()
     for cp in row_loads:
         cp.wait()
 
@@ -456,7 +457,8 @@
 
     def step(i, n):
         slot = lax.rem(i, OUT_SLOTS)
-        act_copy(i, n).wait()
+        for k in range(len(edges) - 1):
+            pl.when(i == edges[k])(act_copy(k).wait)
 
         def wait_old():
             for cp in out_copies(i - OUT_SLOTS, slot, WIDTH):
@@ -504,7 +506,7 @@
             pltpu.VMEM((OUT_SLOTS, d_loc, WIDTH), f32),
             pltpu.VMEM((OUT_SLOTS, d_loc, WIDTH), f32),
             pltpu.VMEM((OUT_SLOTS, WIDTH, d_loc), f32),
-            pltpu.SemaphoreType.DMA((tiles // 2 + 3,)),
+            pltpu.SemaphoreType.DMA((12,)),
             pltpu.SemaphoreType.DMA((3, OUT_SLOTS)),
         ],
         compiler_params=pltpu.CompilerParams(vmem_limit_bytes=62 * 2**20),

time: 137 us -> 137 us (level)
  no operation moved by 1% of the time
where the time goes in v8:
time: 137 us
  Pallas kernels  133 us (97%)
  starting transfers between devices  2.33 us (2%)
    pallas_call x1, Pallas kernels, exchange(): pl.pallas_call(functools.partial(exchange_kernel, tiles), out_shape=(jax....  119 us
    pallas_call x1, Pallas kernels, weight_grads(): pl.pallas_call(functools.partial(grads_kernel, tiles), in_specs=[any_spec...  13.5 us
  transfers between devices with their start and end apart: 1, of which 0 were waited for; matrix products, arithmetic and copies ran while one was open for 0% of the time, Pallas kernels for 10%

profile of v8, /device:TPU:0, one launch (start us, length us, event | category | flops | bytes accessed | tf_op | source)
XLA Modules:
  0.0 136.8 jit_solution(15647194049272623641)
XLA Ops:
  0.6 119.3 %exchange.1 = (bf16[43,3,256,128]{3,2,1,0:T(8,128)(2,1)}, bf16[512,256]{1,0:T(8,128)(2,1)}, bf16[256,512]{1,0:T(8,128)(2,1)}, f32[8,2,2,8,512]{4,3,2,1,0:T(8,128...) custom-call(bf16[2,8,4096]{2,1,0:T(8,128)(2,1)} %x_hbm.1, bf16[2,8,4096]{2,1,0:T(8,128)(2,1)} %dy_hbm.1, ...), custom_call_target="tpu_custom_call" | custom-call | flops 8999999488 | bytes 28000000 | tf_op jit(solution)/shard_map/exchange/pallas_call | solution.py:382
  120.0 2.3 %all-to-all-start = ((f32[16,2,8,512]{3,2,1,0:T(8,128)}), f32[16,2,8,512]{3,2,1,0:T(8,128)S(1)}, u32[]{:S(2)}, u32[]{:S(2)}) async-start(f32[16,2,8,512]{3,2,1,0:T(8,128)} %bitcast.11), calls=%async_computation | async-start | bytes 1048576 | tf_op jit(solution)/shard_map/all_to_all | solution.py:525
  122.3 0.0 copy-start.2
  122.3 0.0 copy-start.3
  122.3 0.0 copy-start
  122.3 0.0 copy-start.1
  122.3 13.5 %weight_grads.1 = (f32[512,5504]{1,0:T(8,128)}, f32[512,5504]{1,0:T(8,128)}, f32[5504,512]{1,0:T(8,128)}) custom-call(bf16[512,256]{1,0:T(8,128)(2,1)} %get-tuple-element.17.xt_hbm, bf16[256,512]{1,0:T(8,128)(2,1)} %get-tuple-element.18.dy_hbm, bf16[43,3,256,128]{3,2,1,0:T(8,128)(2,1)} %get-tuple-element.19.act_hbm), custom_call_target="tpu_custom_call" | custom-call | flops 4328521728 | bytes 44000000 | tf_op jit(solution)/shard_map/weight_grads/pallas_call | solution.py:499
  135.9 0.0 all-to-all-done
  135.9 0.0 copy-done.2
  136.0 0.0 copy-done.3
  136.0 0.0 copy-done
  136.0 0.0 copy-done.1
  136.0 0.7 pad_maximum_fusion
  (4 shorter events, 0.1 us)
Async XLA Ops:
  120.0 15.9 %all-to-all-start = ((f32[16,2,8,512]{3,2,1,0:T(8,128)}), f32[16,2,8,512]{3,2,1,0:T(8,128)S(1)}, u32[]{:S(2)}, u32[]{:S(2)}) async-start(f32[16,2,8,512]{3,2,1,0:T(8,128)} %bitcast.11), calls=%async_computation | async-start | bytes 1048576 | tf_op jit(solution)/shard_map/all_to_all | solution.py:525
  122.3 13.7 %copy-start.2 = (bf16[2,8,4096]{2,1,0:T(8,128)(2,1)S(1)}, bf16[2,8,4096]{2,1,0:T(8,128)(2,1)}, u32[]{:S(2)}) copy-start(bf16[2,8,4096]{2,1,0:T(8,128)(2,1)} %dy_hbm.1) | copy-start | bytes 393220
  122.3 13.7 %copy-start.3 = (bf16[2,8,4096]{2,1,0:T(8,128)(2,1)S(1)}, bf16[2,8,4096]{2,1,0:T(8,128)(2,1)}, u32[]{:S(2)}) copy-start(bf16[2,8,4096]{2,1,0:T(8,128)(2,1)} %x_hbm.1) | copy-start | bytes 393220
  122.3 13.7 %copy-start = (bf16[8,4096]{1,0:T(8,128)(2,1)S(1)}, bf16[8,4096]{1,0:T(8,128)(2,1)}, u32[]{:S(2)}) copy-start(bf16[8,4096]{1,0:T(8,128)(2,1)} %get-tuple-element.14) | copy-start | bytes 196612
  122.3 13.7 %copy-start.1 = (bf16[8,4096]{1,0:T(8,128)(2,1)S(1)}, bf16[8,4096]{1,0:T(8,128)(2,1)}, u32[]{:S(2)}) copy-start(bf16[8,4096]{1,0:T(8,128)(2,1)} %get-tuple-element.16) | copy-start | bytes 196612

commit v9 on v8

--- a/solution.py
+++ b/solution.py
@@ -10,7 +10,7 @@
 MESH = pl.DeviceIdType.MESH
 LANES = 128
 SLOTS = 8
-LATE_SLOTS = 12
+LATE_SLOTS = 11
 DEFER = 6
 LEAD = 2
 LAGS = (3, 3, 2, 2, 2, 1)

time: 137 us -> 137 us (level)
  no operation moved by 1% of the time
where the time goes in v9:
time: 137 us
  Pallas kernels  133 us (97%)
  starting transfers between devices  2.33 us (2%)
    pallas_call x1, Pallas kernels, exchange(): pl.pallas_call(functools.partial(exchange_kernel, tiles), out_shape=(jax....  119 us
    pallas_call x1, Pallas kernels, weight_grads(): pl.pallas_call(functools.partial(grads_kernel, tiles), in_specs=[any_spec...  13.5 us
  transfers between devices with their start and end apart: 1, of which 0 were waited for; matrix products, arithmetic and copies ran while one was open for 0% of the time, Pallas kernels for 10%

profile of v9, /device:TPU:0, one launch (start us, length us, event | category | flops | bytes accessed | tf_op | source)
XLA Modules:
  0.0 136.7 jit_solution(16084134150965784350)
XLA Ops:
  0.6 119.3 %exchange.1 = (bf16[43,3,256,128]{3,2,1,0:T(8,128)(2,1)}, bf16[512,256]{1,0:T(8,128)(2,1)}, bf16[256,512]{1,0:T(8,128)(2,1)}, f32[8,2,2,8,512]{4,3,2,1,0:T(8,128...) custom-call(bf16[2,8,4096]{2,1,0:T(8,128)(2,1)} %x_hbm.1, bf16[2,8,4096]{2,1,0:T(8,128)(2,1)} %dy_hbm.1, ...), custom_call_target="tpu_custom_call" | custom-call | flops 8999999488 | bytes 28000000 | tf_op jit(solution)/shard_map/exchange/pallas_call | solution.py:382
  119.9 2.3 %all-to-all-start = ((f32[16,2,8,512]{3,2,1,0:T(8,128)}), f32[16,2,8,512]{3,2,1,0:T(8,128)S(1)}, u32[]{:S(2)}, u32[]{:S(2)}) async-start(f32[16,2,8,512]{3,2,1,0:T(8,128)} %bitcast.11), calls=%async_computation | async-start | bytes 1048576 | tf_op jit(solution)/shard_map/all_to_all | solution.py:525
  122.3 0.0 copy-start.2
  122.3 0.0 copy-start.3
  122.3 0.0 copy-start
  122.3 0.0 copy-start.1
  122.3 13.5 %weight_grads.1 = (f32[512,5504]{1,0:T(8,128)}, f32[512,5504]{1,0:T(8,128)}, f32[5504,512]{1,0:T(8,128)}) custom-call(bf16[512,256]{1,0:T(8,128)(2,1)} %get-tuple-element.17.xt_hbm, bf16[256,512]{1,0:T(8,128)(2,1)} %get-tuple-element.18.dy_hbm, bf16[43,3,256,128]{3,2,1,0:T(8,128)(2,1)} %get-tuple-element.19.act_hbm), custom_call_target="tpu_custom_call" | custom-call | flops 4328521728 | bytes 44000000 | tf_op jit(solution)/shard_map/weight_grads/pallas_call | solution.py:499
  135.8 0.0 all-to-all-done
  135.9 0.0 copy-done.2
  136.0 0.0 copy-done.3
  136.0 0.0 copy-done
  136.0 0.0 copy-done.1
  136.0 0.7 pad_maximum_fusion
  (4 shorter events, 0.1 us)
Async XLA Ops:
  119.9 15.9 %all-to-all-start = ((f32[16,2,8,512]{3,2,1,0:T(8,128)}), f32[16,2,8,512]{3,2,1,0:T(8,128)S(1)}, u32[]{:S(2)}, u32[]{:S(2)}) async-start(f32[16,2,8,512]{3,2,1,0:T(8,128)} %bitcast.11), calls=%async_computation | async-start | bytes 1048576 | tf_op jit(solution)/shard_map/all_to_all | solution.py:525
  122.3 13.7 %copy-start.2 = (bf16[2,8,4096]{2,1,0:T(8,128)(2,1)S(1)}, bf16[2,8,4096]{2,1,0:T(8,128)(2,1)}, u32[]{:S(2)}) copy-start(bf16[2,8,4096]{2,1,0:T(8,128)(2,1)} %dy_hbm.1) | copy-start | bytes 393220
  122.3 13.7 %copy-start.3 = (bf16[2,8,4096]{2,1,0:T(8,128)(2,1)S(1)}, bf16[2,8,4096]{2,1,0:T(8,128)(2,1)}, u32[]{:S(2)}) copy-start(bf16[2,8,4096]{2,1,0:T(8,128)(2,1)} %x_hbm.1) | copy-start | bytes 393220
  122.3 13.7 %copy-start = (bf16[8,4096]{1,0:T(8,128)(2,1)S(1)}, bf16[8,4096]{1,0:T(8,128)(2,1)}, u32[]{:S(2)}) copy-start(bf16[8,4096]{1,0:T(8,128)(2,1)} %get-tuple-element.14) | copy-start | bytes 196612
  122.3 13.7 %copy-start.1 = (bf16[8,4096]{1,0:T(8,128)(2,1)S(1)}, bf16[8,4096]{1,0:T(8,128)(2,1)}, u32[]{:S(2)}) copy-start(bf16[8,4096]{1,0:T(8,128)(2,1)} %get-tuple-element.16) | copy-start | bytes 196612
